TPU v7x, 128 devices: a whole 4x4x4 slice. The times are simulated.
128 devices in a mesh: data: 1, cols: 16 (over z, y), model: 8 (over x, core).
Axes of the slice: x: 4, y: 4, z: 4, core: 2. Of those that a mesh axis runs over, the one named last changes fastest.
Arguments:
- x_in: bfloat16 [4, 128, 128, 512], P('data', None, None, ('model', 'cols'))
- w_conv1: bfloat16 [3, 3, 512, 512], P(None, None, ('model', 'cols'))
- b_conv1: float32 [512], replicated
- w_conv2: bfloat16 [3, 3, 512, 512], replicated
- b_conv2: float32 [512], replicated
Outputs:
- output: float32 [4, 128, 128, 512], P('data', 'model', 'cols')
All inputs are finite; a program needn't handle non-finite values.
Results may differ from a plain program's by a relative error of at most 0.001.
Values are sent between devices in bfloat16 or wider.
A program may use at most 1 GiB of HBM per device.

v0:
```python
import jax
import jax.numpy as jnp
from jax import lax
from jax.sharding import PartitionSpec as P

CONV_DIMS = ("NHWC", "HWIO", "NHWC")
GROUP_AXES = ("model", "cols")


def halo_tiles(full, n_rows, n_cols):
    batch, height, width, channels = full.shape
    tile_h = height // n_rows
    tile_w = width // n_cols
    blocks = full.reshape(batch, n_rows, tile_h, width, channels)
    zero_row = jnp.zeros((batch, 1, width, channels), full.dtype)
    above = jnp.concatenate([zero_row, blocks[:, :-1, tile_h - 1]], axis=1)
    below = jnp.concatenate([blocks[:, 1:, 0], zero_row], axis=1)
    row_ext = jnp.concatenate([above[:, :, None], blocks, below[:, :, None]], axis=2)
    grid = row_ext.reshape(batch, n_rows, tile_h + 2, n_cols, tile_w, channels)
    zero_col = jnp.zeros((batch, n_rows, tile_h + 2, 1, channels), full.dtype)
    left = jnp.concatenate([zero_col, grid[:, :, :, :-1, tile_w - 1]], axis=3)
    right = jnp.concatenate([grid[:, :, :, 1:, 0], zero_col], axis=3)
    windows = jnp.concatenate([left[:, :, :, :, None], grid, right[:, :, :, :, None]], axis=4)
    windows = windows.transpose(1, 3, 0, 2, 4, 5)
    return windows.reshape(n_rows * n_cols, batch, tile_h + 2, tile_w + 2, channels)


def bias_relu(z_tile, bias, row_idx, col_idx, height, width):
    tile_h = z_tile.shape[1] - 2
    tile_w = z_tile.shape[2] - 2
    rows_at = row_idx * tile_h - 1 + jnp.arange(tile_h + 2)
    cols_at = col_idx * tile_w - 1 + jnp.arange(tile_w + 2)
    row_ok = (rows_at >= 0) & (rows_at < height)
    col_ok = (cols_at >= 0) & (cols_at < width)
    inside = row_ok[:, None, None] & col_ok[None, :, None]
    return jnp.where(inside, jnp.maximum(z_tile + bias, 0.0), 0.0).astype(jnp.bfloat16)


def solution(mesh):
    n_rows = mesh.shape["model"]
    n_cols = mesh.shape["cols"]

    def run_local(x_in, w_conv1, b_conv1, w_conv2, b_conv2):
        height = x_in.shape[1]
        width = x_in.shape[2]
        part_sum = lax.conv_general_dilated(x_in, w_conv1, (1, 1), "SAME", dimension_numbers=CONV_DIMS, preferred_element_type=jnp.float32)
        windows = halo_tiles(part_sum, n_rows, n_cols)
        z_tile = lax.psum_scatter(windows, GROUP_AXES, scatter_dimension=0, tiled=False)
        act_tile = bias_relu(z_tile, b_conv1, lax.axis_index("model"), lax.axis_index("cols"), height, width)
        out_tile = lax.conv_general_dilated(act_tile, w_conv2, (1, 1), "VALID", dimension_numbers=CONV_DIMS, preferred_element_type=jnp.float32)
        return out_tile + b_conv2

    return jax.shard_map(
        run_local,
        mesh=mesh,
        in_specs=(P("data", None, None, GROUP_AXES), P(None, None, GROUP_AXES, None), P(), P(), P()),
        out_specs=P("data", "model", "cols", None),
        check_vma=False,
    )
```

profile of v0, /device:TPU:1, one launch (start us, length us, event | category | flops | bytes accessed | tf_op | source)
XLA Modules:
  0.0 2179.8 jit_solution(14319879975613851374)
XLA Ops:
  6.5 0.0 copy-start
  6.5 0.0 all-reduce.7.cloned.1.call-start
  6.5 1.5 copy.71
  8.1 0.2 pad.4.clone
  8.3 0.3 fusion.8
  8.6 3.5 copy.53
  12.1 0.0 copy-done
  12.1 47.6 %broadcast_select_fusion = f32[128,32,17,512]{3,1,2,0:T(8,128)} fusion(pred[32,17]{0,1:T(8,128)(4,1)} %constant.42, bf16[128,32,19,4]{1,3,2,0:T(4,128)(2,1)S(1)} %copy.53, bf16[3,3,4,512]{3,2,1,0:T(4,128)(2,1)S(1)} %copy-done), kind=kOutput, calls=%fused_computation.1 | convolution fusion | flops 2589196288 | bytes 143266336 | tf_op jit(solution)/shard_map/conv_general_dilated | solution.py:46
  59.7 115.5 %copy.54 = f32[128,32,17,512]{3,0,2,1:T(8,128)} copy(f32[128,32,17,512]{3,1,2,0:T(8,128)} %broadcast_select_fusion) | data formatting | bytes 285212672 | tf_op jit(solution)/shard_map/conv_general_dilated | solution.py:46
  175.2 130.1 %slice_bitcast_fusion = (f32[4,128,128,512]{3,1,2,0:T(8,128)}, f32[128,4,128,512]{3,0,2,1:T(8,128)}) fusion(f32[128,4,136,512]{3,0,2,1:T(8,128)} %bitcast.3), kind=kLoop, calls=%fused_computation.27 | loop fusion | bytes 402653184 | tf_op jit(solution)/shard_map/conv_general_dilated | solution.py:46
  305.3 42.1 %fusion.11 = (f32[4,7,1,128,512]{4,2,1,3,0:T(1,128)}, f32[4,7,1,128,512]{4,2,1,3,0:T(1,128)}) fusion(f32[4,8,16,128,512]{4,2,1,3,0:T(8,128)} %bitcast.5), kind=kLoop, calls=%fused_computation.28 | loop fusion | bytes 29360128 | tf_op jit(solution)/shard_map/slice | solution.py:16
  347.3 13.2 copy_bitcast_fusion.2
  360.5 0.0 slice-start
  360.5 0.0 slice-start.1
  360.5 8.0 pad_bitcast_fusion
  368.5 0.0 slice-done
  368.5 0.0 slice-done.1
  368.5 4.3 pad_bitcast_fusion.1
  372.8 108.9 %copy.56 = f32[4,128,128,512]{3,2,1,0:T(8,128)} copy(f32[4,128,128,512]{3,1,2,0:T(8,128)} %get-tuple-element.7) | data formatting | bytes 268435456 | tf_op jit(solution)/shard_map/conv_general_dilated | solution.py:46
  481.7 96.2 %pad_maximum_fusion.2 = (f32[4,8,18,15,1,512]{5,4,3,2,1,0:T(1,128)}, f32[4,8,18,15,1,512]{5,4,3,2,1,0:T(1,128)}) fusion(f32[4,8,1,16,8,512]{5,4,3,2,1,0:T(8,128)} %pad_bitcast_fusion, f32[4,8,16,16,8,512]{5,4,3,2,1,0:T(8,128)} %bitcast.9, f32[4,8,1,16,8,512]{5,4,3,2,1,0:T(8,128)} %pad_bitcast_fusion.1), kind=kLoop, calls=%fused_computation.6 | loop fusion | flops 17694720 | bytes 186384384 | tf_op jit(solution)/shard_map/slice | solution.py:21
  577.9 8.9 copy.77
  586.8 7.7 concatenate.31
  594.5 16.9 broadcast_in_dim.11
  611.4 8.9 copy.76
  620.3 9.2 concatenate.32
  629.4 17.0 broadcast_in_dim.12
  646.4 162.0 %maximum_bitcast_fusion = f32[8,16,4,18,10,512]{5,4,1,3,0,2:T(8,128)} fusion(f32[4,8,18,16,1,512]{5,4,3,2,1,0:T(1,128)} %broadcast_in_dim.12, f32[4,8,1,16,8,512]{5,4,3,2,1,0:T(8,128)} %pad_bitcast_fusion, f32[4,8,16,16,8,512]{5,4,3,2,1,0:T(8,128)} %bitcast.9, f32[4,8,1,16,8,512]{5,4,3,2,1,0:T(8,128)} %pad_bitcast_fusion.1, ...), kind=kLoop, calls=%fused_computation | loop fusion | flops 188743680 | bytes 377487360 | tf_op jit(solution)/shard_map/transpose | solution.py:24
  808.4 180.7 %copy.62 = f32[8,16,4,18,10,512]{5,1,0,4,3,2:T(8,128)} copy(f32[8,16,4,18,10,512]{5,4,1,3,0,2:T(8,128)} %maximum_bitcast_fusion) | data formatting | bytes 377487360 | tf_op jit(solution)/shard_map/transpose | solution.py:24
  989.1 204.7 %copy.63 = f32[128,4,18,10,512]{4,1,3,2,0:T(4,128)} copy(f32[128,4,18,10,512]{4,0,3,2,1:T(8,128)} %bitcast.16) | data formatting | bytes 377487360 | tf_op jit(solution)/shard_map/reshape | solution.py:25
  1193.8 0.0 copy-start.4
  1193.8 0.0 copy-start.2
  1193.8 0.0 copy-start.3
  1193.8 0.0 all-reduce.7.cloned.1.call-update
  1193.8 0.6 copy-done.4
  1194.4 0.6 dynamic-slice
  1195.0 0.1 broadcast_and_fusion
  1195.1 968.8 %all-reduce.7.cloned.1.call-done = f32[128,4,18,10,512]{4,1,3,2,0:T(4,128)} async-done(((f32[128,4,18,10,512]{4,1,3,2,0:T(4,128)}), f32[128,4,18,10,512]{4,1,3,2,0:T(4,128)}) %all-reduce.7.cloned.1.call-update) | async-done | bytes 188743696
  2163.9 0.0 copy-start.1
  2163.9 0.0 copy-done.2
  2163.9 0.0 copy-done.3
  2163.9 7.7 convolution_add_fusion
  2171.6 1.3 copy.64
  2172.9 0.0 copy-done.1
  (4 shorter events, 0.0 us)
Async XLA Ops:
  6.5 5.5 copy-start
  6.5 2157.4 %all-reduce.7.cloned.1.call-start = ((), (), s32[]{:S(2)}) async-start(), calls=%async_computation | async-start | bytes 377487360
  360.5 8.0 slice-start
  360.5 8.0 slice-start.1
  1193.8 0.7 copy-start.4
  1193.8 970.1 %copy-start.2 = (f32[512]{0:T(512)S(1)}, f32[512]{0:T(512)}, u32[]{:S(2)}) copy-start(f32[512]{0:T(512)} %param.7) | copy-start | bytes 6148
  1193.8 970.1 %copy-start.3 = (f32[512]{0:T(512)S(1)}, f32[512]{0:T(512)}, u32[]{:S(2)}) copy-start(f32[512]{0:T(512)} %param.9) | copy-start | bytes 6148
  2163.9 9.0 copy-start.1
Sparse Core Ops, SparseCore 0:
  1194.0 969.8 all-reduce.6
where the time goes:
time: 2180 us
  waiting for transfers between devices  969 us (44%)
  local copies, waits for them, and re-layouts  884 us (41%)
  other arithmetic  259 us (12%)
  matrix products  55.3 us (3%)
    unnamed x2, waiting for transfers between devices  969 us
    conv_general_dilated x5, local copies, waits for them, and re-layouts, run_local(): lax.conv_general_dilated(x_in, w_conv1, (1, 1), 'SAME', dimension_numbers...  358 us
    reshape x1, local copies, waits for them, and re-layouts, halo_tiles(): windows.reshape(n_rows * n_cols, batch, tile_h + 2, tile_w + 2, channels)  205 us
    transpose x1, local copies, waits for them, and re-layouts, halo_tiles(): windows = windows.transpose(1, 3, 0, 2, 4, 5)  181 us
    transpose x1, other arithmetic, halo_tiles(): windows = windows.transpose(1, 3, 0, 2, 4, 5)  162 us
    slice x1, other arithmetic, halo_tiles(): left = jnp.concatenate([zero_col, grid[:, :, :, :-1, tile_w - 1]], axis=3)  96.2 us
    conv_general_dilated x1, matrix products, run_local(): lax.conv_general_dilated(x_in, w_conv1, (1, 1), 'SAME', dimension_numbers...  47.6 us
  transfers between devices with their start and end apart: 1, of which 1 were waited for; matrix products, arithmetic and copies ran while one was open for 0% of the time, Pallas kernels for 0%

commit v1 on v0

v1 whole, which is shorter than its diff:
```python
import jax
import jax.numpy as jnp
from jax import lax
from jax.experimental import pallas as pl
from jax.experimental.pallas import tpu as pltpu
from jax.sharding import PartitionSpec as P

GROUP_AXES = ("model", "cols")
MESH = pl.DeviceIdType.MESH
BF16 = jnp.bfloat16
F32 = jnp.float32
CHANS = 512
LANES = 128
CUT = 96
CHUNKS = ((0,), (1,), (2,))
VMEM_LIMIT = 36 * 2**20
ORDERS = (("y", "z", "x"), ("z", "x", "y"), ("x", "y", "z"))


def one_hot(shape, col_of_row):
    rows = lax.broadcasted_iota(jnp.int32, shape, 0)
    cols = lax.broadcasted_iota(jnp.int32, shape, 1)
    return jnp.where(cols == col_of_row(rows), 1.0, 0.0).astype(BF16)


def column_of(r):
    w = (r % 272) // 4 * 2 - 1 + r // 272
    return jnp.where((w >= 0) & (w < LANES), (r % 4) * LANES + w, -1)


def pack_windows(xv, a_scr, pack):
    to_lanes = one_hot((CHANS, CHANS), lambda r: (r % 4) * LANES + ((r % LANES) // 4) * 4 + r // LANES)
    to_rows = one_hot((544, CHANS), column_of)
    for blk in range(4):
        part = jnp.concatenate([xv[n, 32 * blk : 32 * blk + 32].reshape(LANES, LANES) for n in range(4)], axis=0)
        turned = lax.dot_general(part, to_lanes, (((0,), (0,)), ((), ())), preferred_element_type=F32).astype(BF16)
        for c in range(4):
            a_scr[c * LANES : (c + 1) * LANES, blk * LANES : (blk + 1) * LANES] = turned[:, c * LANES : (c + 1) * LANES]
    mixed = jnp.dot(to_rows, a_scr[...], preferred_element_type=F32)
    for blk in range(4):
        two = [mixed[272 * p : 272 * p + 272, blk * LANES : (blk + 1) * LANES] for p in range(2)]
        for half in range(2):
            tile = jnp.concatenate([t[:, 64 * half : 64 * half + 64] for t in two], axis=1).astype(BF16)
            pack[2 * blk + half] = tile.reshape(68, 4, LANES)


def kernel(
    x_hbm, w1_hbm, w2_hbm, b1_hbm, b2_hbm, o_ref,
    xv, w1v, w2v, b1v, b2v, a_scr, pack, got, x0, x1, x2, edge, side, w1g, z_acc, y0, y1, y2,
    load_sem, xs_send, xs_recv, halo_send, halo_recv, step_send, step_recv,
):
    m = lax.axis_index("model")
    q = lax.axis_index("cols")
    me = {"x": m // 2, "z": q // 4, "y": q % 4}
    core = m % 2
    parts = range(3)
    barrier = pltpu.get_barrier_semaphore()

    at_model = [[(me["x"] + dx) % 4 * 2 + (core + dk) % 2 for dk in range(2)] for dx in range(4)]
    at_cols = [[(me["z"] + dz) % 4 * 4 + (me["y"] + dy) % 4 for dy in range(4)] for dz in range(4)]
    others = [(dx, dz, dy, dk) for dx in range(4) for dz in range(4) for dy in range(4) for dk in range(2)]
    others = sorted(others[1:], key=lambda d: (sum(d[:3]) % 4, d))

    def away(d):
        return {"model": at_model[d[0]][d[3]], "cols": at_cols[d[1]][d[2]]}

    loads = [
        pltpu.make_async_copy(src, dst, load_sem.at[k])
        for k, (src, dst) in enumerate(
            ((x_hbm, xv), (w1_hbm, w1v), (w2_hbm, w2v.at[pl.ds(0, 4608)]), (b1_hbm, b1v), (b2_hbm, b2v))
        )
    ]
    for load in loads:
        load.start()
    with jax.named_scope("announce"):
        for d in sorted(others, key=lambda d: -sum(min(o, 4 - o) for o in d[:3])):
            pl.semaphore_signal(barrier, inc=1, device_id=away(d), device_id_type=MESH)

    def piece(p, t, v, dws, c, half=None):
        done = ORDERS[p][:t]
        rest = [a for a in "xzy" if a != ORDERS[p][2]]
        at = [v if t < 2 and a == ORDERS[p][t] else (pl.ds(0, 4) if a in done else me[a]) for a in rest]
        if half is not None:
            at[0] = pl.ds(2 * half, 2)
        return w1g.at[p, me[ORDERS[p][2]] if t < 2 else v, c, at[0], at[1], pl.ds(dws[0], len(dws))]

    with jax.named_scope("place_w1"):
        loads[1].wait()
        for p in parts:
            spot = [me[a] for a in "xzy" if a != ORDERS[p][2]]
            for dw in range(3):
                for lt in range(4):
                    tile = w1v[3 * p + dw, :, lt * LANES : (lt + 1) * LANES]
                    w1g[p, me[ORDERS[p][2]], core, spot[0], spot[1], dw, lt] = tile
    with jax.named_scope("wait_x"):
        loads[0].wait()
    with jax.named_scope("pack"):
        pack_windows(xv, a_scr, pack)
    with jax.named_scope("wait_barrier"):
        pl.semaphore_wait(barrier, 127)

    n_steps = [0]
    steps = []

    class Step:
        def __init__(self, size, copies):
            k = n_steps[0]
            n_steps[0] += 1
            sems = dict(send_sem=step_send.at[k], recv_sem=step_recv.at[k], device_id_type=MESH)
            for ref, to in copies:
                pltpu.make_async_remote_copy(src_ref=ref, dst_ref=ref, device_id=to, **sems).start()
            span = got.at[pl.ds(0, size)]
            self.all = pltpu.make_async_remote_copy(
                src_ref=span, dst_ref=span, device_id={"model": at_model[0][1], "cols": q}, **sems
            )
            steps.append(self)

        def land(self):
            self.all.wait_recv()

    def chip(p, t, d, c=0):
        axis = ORDERS[p][t]
        pos = me | {axis: (me[axis] + d) % 4}
        return {"model": pos["x"] * 2 + (core + c) % 2, "cols": pos["z"] * 4 + pos["y"]}

    def spread(t, size):
        return Step(size, [(piece(p, t, me[ORDERS[p][t]], parts, core), chip(p, t, d)) for p in parts for d in (1, 3, 2)])

    def plane(p, d):
        return (me[ORDERS[p][2]] + d) % 4

    def hand_over(pieces, size):
        return Step(size, [(ref, {"model": at_model[0][1], "cols": q}) for ref in pieces])

    def send_windows(first, last):
        for d in others[first:last]:
            to = away(d)
            pltpu.make_async_remote_copy(
                src_ref=pack.at[to["model"], pl.ds(4 * to["cols"], 5)],
                dst_ref=got.at[pl.ds(5 * mine, 5)],
                send_sem=xs_send,
                recv_sem=xs_recv,
                device_id=to,
                device_id_type=MESH,
            ).start()

    mine = ((core * 4 + me["x"]) * 4 + me["z"]) * 4 + me["y"]
    with jax.named_scope("send_first"):
        first = spread(0, 108)
        for pair in range(5):
            got[5 * mine + pair] = pack[m, 4 * q + pair]
        send_windows(0, CUT)
    with jax.named_scope("wait_first"):
        first.land()
    with jax.named_scope("send_second"):
        second = spread(1, 432)
        send_windows(CUT, 127)
    with jax.named_scope("wait_second"):
        second.land()
    last, passed, lent, lent_on = {}, {}, {}, {}

    def send_plane(dws):
        size = 384 * len(dws)
        last[dws] = Step(size, [(piece(p, 2, plane(p, 0), dws, core), chip(p, 2, d)) for p in parts for d in (1, 3)])

    def pass_on(dws):
        size = 384 * len(dws)
        with jax.named_scope(f"wait_last{dws[0]}"):
            last[dws].land()
        on = [(piece(p, 2, plane(p, 4 - d), dws, core, d // 2), chip(p, 2, d)) for p in parts for d in (1, 3)]
        passed[dws] = Step(size // 2, on)
        lent[dws] = hand_over([piece(p, 2, plane(p, d), dws, core) for p in parts for d in (1, 3)], size)

    def finish(dws):
        with jax.named_scope(f"wait_passed{dws[0]}"):
            passed[dws].land()
        lent_on[dws] = hand_over([piece(p, 2, plane(p, 2), dws, core) for p in parts], 192 * len(dws))

    with jax.named_scope("send_third"):
        for dws in CHUNKS:
            send_plane(dws)
        own = hand_over([piece(p, 2, plane(p, 0), parts, core) for p in parts], 576)

    span = got.at[pl.ds(0, 635)]
    everything = pltpu.make_async_remote_copy(
        src_ref=span, dst_ref=span, send_sem=xs_send, recv_sem=xs_recv, device_id=chip(0, 0, 0, 1), device_id_type=MESH
    )
    with jax.named_scope("wait_windows"):
        everything.wait_recv()
    xs, ys = (x0, x1, x2), (y0, y1, y2)
    with jax.named_scope("turn"):
        for pair in range(5):
            for p in parts:
                rows = []
                for v in range(4):
                    for at in (pair, 320 + pair):
                        if p == 0:
                            rows.append(got[at + 80 * v : at + 80 * v + 80 : 5])
                        elif p == 1:
                            rows.append(got[at + 5 * v : at + 316 : 20])
                        else:
                            rows += [got[at + 80 * a + 20 * v : at + 80 * a + 20 * v + 20 : 5] for a in range(4)]
                rows = jnp.concatenate([r.reshape(-1, LANES) for r in rows], axis=0).T
                for odd in range(2):
                    main = rows[64 * odd : 64 * odd + 64]
                    xs[p][2 * pair + odd, 8 - 4 * p : 72 - 4 * p] = main
                    if p == 1:
                        edge[0, 2 * pair + odd] = main[60:64]
                        edge[1, 2 * pair + odd] = main[0:4]
    halo = []
    for src, dst, d in (
        (x0.at[:, pl.ds(64, 8)], x0.at[:, pl.ds(0, 8)], 1),
        (x2.at[:, pl.ds(0, 8)], x2.at[:, pl.ds(64, 8)], 7),
        (edge.at[0], edge.at[2], 1),
        (edge.at[1], edge.at[3], 7),
    ):
        halo.append(
            pltpu.make_async_remote_copy(
                src_ref=src,
                dst_ref=dst,
                send_sem=halo_send.at[len(halo)],
                recv_sem=halo_recv.at[len(halo)],
                device_id={"model": (m + d) % 8, "cols": q},
                device_id_type=MESH,
            )
        )
        halo[-1].start()

    def conv1(dws, places, spans):
        total = None
        for p in parts:
            at = [plane(p, d) for d in places]
            lanes = [pl.ds(pl.multiple_of(LANES * v, LANES), LANES) for v in at]
            for dw in dws:
                right = [[w1g[p, v, :, :, :, dw, lt].reshape(LANES, LANES) for lt in range(4)] for v in at]
                right = jnp.concatenate([jnp.concatenate(r, axis=1) for r in right], axis=0)
                left = [jnp.concatenate([xs[p][dw : dw + 8, rows, s] for s in lanes], axis=-1) for rows in spans]
                left = jnp.concatenate(left, axis=1).reshape(-1, 256)
                term = jnp.dot(left, right, preferred_element_type=F32)
                total = term if total is None else total + term
        return total.reshape(8, -1, CHANS)

    every, top_rows, inner, low_rows = pl.ds(0, 72), pl.ds(0, 8), pl.ds(8, 56), pl.ds(64, 8)

    def near(dws):
        with jax.named_scope(f"wait_lent{dws[0]}"):
            lent[dws].land()
        with jax.named_scope(f"near{dws[0]}"):
            top = conv1(dws, (3, 1), (inner,))
            z_acc[:, inner] = top if dws == CHUNKS[0] else z_acc[:, inner] + top

    def rim():
        with jax.named_scope("rim"):
            top = conv1(parts, (3, 1), (top_rows, low_rows))
            z_acc[:, top_rows] = top[:, :8]
            z_acc[:, low_rows] = top[:, 8:]

    def far(dws):
        with jax.named_scope(f"wait_lent_on{dws[0]}"):
            lent_on[dws].land()
        with jax.named_scope(f"far{dws[0]}"):
            total = z_acc[...] + conv1(dws, (0, 2), (every,))
            if dws != CHUNKS[-1]:
                z_acc[...] = total
                return
            act = jnp.maximum(total + b1v[...], 0.0).astype(BF16)
            side[0], side[1] = act[0], act[7]
            for dh in range(3):
                ys[dh][1:9] = act[:, 4 * dh : 4 * dh + 64]
            clear(m == 0, (y0,), pl.ds(1, 8), pl.ds(0, 4))
            clear(m == 7, (y2,), pl.ds(1, 8), pl.ds(60, 4))

    def clear(at_edge, refs, cols, rows):
        @pl.when(at_edge)
        def _():
            for ref in refs:
                ref[cols, rows] = jnp.zeros((cols.size, rows.size, CHANS), BF16)

    def trade_sides():
        for k, d in enumerate((15, 1)):
            halo.append(
                pltpu.make_async_remote_copy(
                    src_ref=side.at[k],
                    dst_ref=side.at[2 + k],
                    send_sem=halo_send.at[4 + k],
                    recv_sem=halo_recv.at[4 + k],
                    device_id={"model": m, "cols": (q + d) % 16},
                    device_id_type=MESH,
                )
            )
            halo[-1].start()

    def take_sides():
        with jax.named_scope("wait_sides"):
            for copy in halo[4:]:
                copy.wait_recv()
        for k, col in enumerate((9, 0)):
            for dh in range(3):
                ys[dh][col] = side[2 + k, 4 * dh : 4 * dh + 64]
            outer = pl.ds(col, 1)
            clear(m == 0, (y0,), outer, pl.ds(0, 4))
            clear(m == 7, (y2,), outer, pl.ds(60, 4))
            clear(q == (15, 0)[k], ys, outer, pl.ds(0, 64))

    def conv2(spans):
        total = None
        for dh in range(3):
            for dw in range(3):
                tap = 3 * dh + dw
                left = [ys[dh][dw + first : dw + last].reshape(-1, CHANS) for first, last in spans]
                left = jnp.concatenate(left, axis=0)
                term = jnp.dot(left, w2v[CHANS * tap : CHANS * tap + CHANS, :], preferred_element_type=F32)
                total = term if total is None else total + term
        return total + b2v[...]

    pass_on(CHUNKS[0])
    pass_on(CHUNKS[1])
    pass_on(CHUNKS[2])
    near(CHUNKS[0])
    near(CHUNKS[1])
    near(CHUNKS[2])
    finish(CHUNKS[0])
    with jax.named_scope("wait_halo"):
        for copy in halo[:4]:
            copy.wait_recv()

    @pl.when(m == 0)
    def _():
        x0[:, 0:8] = jnp.zeros((10, 8, CHANS), BF16)
        x1[:, 0:4] = jnp.zeros((10, 4, CHANS), BF16)

    @pl.when(m > 0)
    def _():
        x1[:, 0:4] = edge[2]

    @pl.when(m == 7)
    def _():
        x2[:, 64:72] = jnp.zeros((10, 8, CHANS), BF16)
        x1[:, 68:72] = jnp.zeros((10, 4, CHANS), BF16)

    @pl.when(m < 7)
    def _():
        x1[:, 68:72] = edge[3]

    rim()
    finish(CHUNKS[1])
    finish(CHUNKS[2])
    with jax.named_scope("wait_own_w2"):
        own.land()
        for load in loads[2:]:
            load.wait()
    far(CHUNKS[0])
    far(CHUNKS[1])
    far(CHUNKS[2])
    trade_sides()
    with jax.named_scope("conv2_in"):
        o_ref[64:448] = conv2(((1, 7),))
    take_sides()
    with jax.named_scope("conv2_out"):
        outer = conv2(((0, 1), (7, 8)))
        o_ref[0:64], o_ref[448:CHANS] = outer[:64], outer[64:]

    with jax.named_scope("wait_sends"):
        everything.wait_send()
        for step in steps:
            step.all.wait_send()
        for copy in halo:
            copy.wait_send()


def arrange(sum_ref, o_hbm, turned, sems):
    copies = []
    for g in range(4):
        rows = jnp.transpose(sum_ref[:, 16 * g : 16 * g + 16], (1, 0, 2))
        for h in range(4):
            for image in range(4):
                turned[g, image, h] = rows[4 * h + image]
        copies.append(pltpu.make_async_copy(turned.at[g], o_hbm.at[:, pl.ds(4 * g, 4)], sems.at[g]))
        copies[-1].start()
    for copy in copies:
        copy.wait()


def solution(mesh):
    scratch = [
        pltpu.VMEM((4, LANES, 4, LANES), BF16),
        pltpu.VMEM((9, 4, CHANS), BF16),
        pltpu.VMEM((4616, CHANS), BF16),
        pltpu.VMEM((1, CHANS), F32),
        pltpu.VMEM((1, CHANS), F32),
        pltpu.VMEM((CHANS, CHANS), BF16),
        pltpu.VMEM((8, 68, 4, LANES), BF16),
        pltpu.VMEM((640, 4, LANES), BF16),
        *[pltpu.VMEM((10, 72, CHANS), BF16) for _ in range(3)],
        pltpu.VMEM((4, 10, 4, CHANS), BF16),
        pltpu.VMEM((4, 72, CHANS), BF16),
        pltpu.VMEM((3, 4, 2, 4, 4, 3, 4, 4, LANES), BF16),
        pltpu.VMEM((8, 72, CHANS), F32),
        *[pltpu.VMEM((10, 64, CHANS), BF16) for _ in range(3)],
        pltpu.SemaphoreType.DMA((5,)),
        pltpu.SemaphoreType.DMA,
        pltpu.SemaphoreType.DMA,
        pltpu.SemaphoreType.DMA((6,)),
        pltpu.SemaphoreType.DMA((6,)),
        pltpu.SemaphoreType.DMA((15,)),
        pltpu.SemaphoreType.DMA((15,)),
    ]
    vmem = pl.BlockSpec(memory_space=pltpu.VMEM)
    anywhere = pl.BlockSpec(memory_space=pl.ANY)

    def run_local(x_in, w_conv1, b_conv1, w_conv2, b_conv2):
        sums = pl.pallas_call(
            kernel,
            out_shape=jax.ShapeDtypeStruct((CHANS, CHANS), F32),
            in_specs=[anywhere] * 5,
            out_specs=vmem,
            scratch_shapes=scratch,
            compiler_params=pltpu.CompilerParams(collective_id=0, has_side_effects=True, vmem_limit_bytes=VMEM_LIMIT),
            name="two_convs",
        )(
            *(
                pltpu.with_memory_space_constraint(a, pltpu.HBM)
                for a in (
                    x_in.transpose(0, 1, 3, 2),
                    w_conv1.reshape(9, 4, CHANS),
                    w_conv2.reshape(4608, CHANS),
                    b_conv1.reshape(1, CHANS),
                    b_conv2.reshape(1, CHANS),
                )
            )
        )
        return pl.pallas_call(
            arrange,
            out_shape=jax.ShapeDtypeStruct((4, 16, 8, CHANS), F32),
            in_specs=[vmem],
            out_specs=anywhere,
            scratch_shapes=[pltpu.VMEM((4, 4, 4, 8, CHANS), F32), pltpu.SemaphoreType.DMA((4,))],
            compiler_params=pltpu.CompilerParams(vmem_limit_bytes=8 * 2**20),
            name="arrange",
        )(sums.reshape(8, 64, CHANS))

    return jax.shard_map(
        run_local,
        mesh=mesh,
        in_specs=(P("data", None, None, GROUP_AXES), P(None, None, GROUP_AXES, None), P(), P(), P()),
        out_specs=P("data", "model", "cols", None),
        check_vma=False,
    )
```

time: 2180 us -> 41.6 us (0.02)
  the two profiles are of different devices: /device:TPU:1 before, /device:TPU:2 now
where the time goes in v1:
time: 41.6 us; the launch traced here: 41.5 us
  Pallas kernels  41.5 us (100%)
    pallas_call x1, Pallas kernels, run_local(): pl.pallas_call(kernel, out_shape=jax.ShapeDtypeStruct((CHANS, CHANS), F32...  40.5 us
    pallas_call x1, Pallas kernels, run_local(): pl.pallas_call(arrange, out_shape=jax.ShapeDtypeStruct((4, 16, 8, CHANS),...  1.05 us

profile of v1, /device:TPU:2, one launch (start us, length us, event | category | flops | bytes accessed | tf_op | source)
XLA Modules:
  0.0 41.5 jit_solution(2461855221872326947)
XLA Ops:
  0.0 40.5 %two_convs.1 = f32[512,512]{1,0:T(8,128)S(1)} custom-call(bf16[4,128,4,128]{3,2,1,0:T(4,128)(2,1)} %bitcast.8, bf16[9,4,512]{2,1,0:T(4,128)(2,1)} %bitcast.9, bf16[4608,512]{1,0:T(8,128)(2,1)} %bitcast.7, f32[1,512]{1,0:T(1,128)} %bitcast.10, f32[1,512]{1,0:T(1,128)} %bitcast.11), custom_call_target="tpu_custom_call" | custom-call | tf_op jit(solution)/shard_map/two_convs/pallas_call | solution.py:412
  40.5 1.0 %arrange.1 = f32[4,16,8,512]{3,2,1,0:T(8,128)} custom-call(f32[8,64,512]{2,1,0:T(8,128)S(1)} %bitcast.6), custom_call_target="tpu_custom_call" | custom-call | tf_op jit(solution)/shard_map/arrange/pallas_call | solution.py:432

commit v2 on v1

v2 whole, which is shorter than its diff:
```python
import jax
import jax.numpy as jnp
from jax import lax
from jax.experimental import pallas as pl
from jax.experimental.pallas import tpu as pltpu
from jax.sharding import PartitionSpec as P

GROUP_AXES = ("model", "cols")
MESH = pl.DeviceIdType.MESH
BF16 = jnp.bfloat16
F32 = jnp.float32
CHANS = 512
LANES = 128
CUTS = (96, 127)
VMEM_LIMIT = 36 * 2**20
ORDERS = (("y", "z", "x"), ("z", "x", "y"), ("x", "y", "z"))


def one_hot(shape, col_of_row):
    rows = lax.broadcasted_iota(jnp.int32, shape, 0)
    cols = lax.broadcasted_iota(jnp.int32, shape, 1)
    return jnp.where(cols == col_of_row(rows), 1.0, 0.0).astype(BF16)


def pack_windows(xv, a_scr, pack):
    to_lanes = one_hot((CHANS, CHANS), lambda r: (r % 4) * LANES + ((r % LANES) // 4) * 4 + r // LANES)
    to_rows = one_hot((CHANS, CHANS), lambda r: (r % 4) * LANES + ((r % 256) // 4) * 2 + r // 256)
    for blk in range(4):
        part = jnp.concatenate([xv[n, 32 * blk : 32 * blk + 32].reshape(LANES, LANES) for n in range(4)], axis=0)
        turned = lax.dot_general(part, to_lanes, (((0,), (0,)), ((), ())), preferred_element_type=F32).astype(BF16)
        for c in range(4):
            a_scr[c * LANES : (c + 1) * LANES, blk * LANES : (blk + 1) * LANES] = turned[:, c * LANES : (c + 1) * LANES]
    mixed = jnp.dot(to_rows, a_scr[...], preferred_element_type=F32)
    for blk in range(4):
        even = mixed[0:256, blk * LANES : (blk + 1) * LANES]
        odd = mixed[256:CHANS, blk * LANES : (blk + 1) * LANES]
        for half in range(2):
            s = slice(64 * half, 64 * half + 64)
            tile = jnp.concatenate([even[:, s], odd[:, s]], axis=1).astype(BF16)
            pack[2 * blk + half, 1:65] = tile.reshape(64, 4, LANES)
    edge = jnp.zeros((8, 1, 4, LANES), BF16)
    pack[:, 0:1] = edge
    pack[:, 65:66] = edge


def kernel(
    x_hbm, w1_hbm, w2_hbm, b1_hbm, b2_hbm, o_ref,
    xv, w1v, w2v, b1v, b2v, a_scr, pack, got, x0, x1, x2, edge, w1g, z_acc, y0, y1, y2, acc2,
    load_sem, xs_send, xs_recv, halo_send, halo_recv, step_send, step_recv,
):
    m = lax.axis_index("model")
    q = lax.axis_index("cols")
    me = {"x": m // 2, "z": q // 4, "y": q % 4}
    core = m % 2
    parts = range(3)
    barrier = pltpu.get_barrier_semaphore()

    at_model = [[(me["x"] + dx) % 4 * 2 + (core + dk) % 2 for dk in range(2)] for dx in range(4)]
    at_cols = [[(me["z"] + dz) % 4 * 4 + (me["y"] + dy) % 4 for dy in range(4)] for dz in range(4)]
    others = [(dx, dz, dy, dk) for dx in range(4) for dz in range(4) for dy in range(4) for dk in range(2)]
    others = sorted(others[1:], key=lambda d: (sum(d[:3]) % 4, d))

    def away(d):
        return {"model": at_model[d[0]][d[3]], "cols": at_cols[d[1]][d[2]]}

    loads = [
        pltpu.make_async_copy(src, dst, load_sem.at[k])
        for k, (src, dst) in enumerate(
            ((x_hbm, xv), (w1_hbm, w1v), (w2_hbm, w2v.at[pl.ds(0, 4608)]), (b1_hbm, b1v), (b2_hbm, b2v))
        )
    ]
    for load in loads:
        load.start()
    with jax.named_scope("announce"):
        for d in sorted(others, key=lambda d: -sum(min(o, 4 - o) for o in d[:3])):
            pl.semaphore_signal(barrier, inc=1, device_id=away(d), device_id_type=MESH)

    def piece(p, t, v, n, c, place=None, half=None):
        done = ORDERS[p][:t]
        rest = [a for a in "xzy" if a != ORDERS[p][2]]
        at = [v if t < 2 and a == ORDERS[p][t] else (pl.ds(0, 4) if a in done else me[a]) for a in rest]
        if half is not None:
            at[0] = pl.ds(2 * half, 2)
        return w1g.at[p, pl.ds(0, 2) if n is None else n, me[ORDERS[p][2]] if t < 2 else v, c, at[0], at[1]]

    with jax.named_scope("place_w1"):
        loads[1].wait()
        for p in parts:
            spot = [me[a] for a in "xzy" if a != ORDERS[p][2]]
            for dw in range(3):
                for lt in range(4):
                    tile = w1v[3 * p + dw, :, lt * LANES : (lt + 1) * LANES]
                    w1g[p, lt // 2, me[ORDERS[p][2]], core, spot[0], spot[1], dw, lt % 2] = tile
    with jax.named_scope("wait_x"):
        loads[0].wait()
    with jax.named_scope("pack"):
        pack_windows(xv, a_scr, pack)
    with jax.named_scope("wait_barrier"):
        pl.semaphore_wait(barrier, 127)

    n_steps = [0]
    steps = []

    class Step:
        def __init__(self, slabs, copies):
            k = n_steps[0]
            n_steps[0] += 1
            sems = dict(send_sem=step_send.at[k], recv_sem=step_recv.at[k], device_id_type=MESH)
            for ref, to in copies:
                pltpu.make_async_remote_copy(src_ref=ref, dst_ref=ref, device_id=to, **sems).start()
            span = got.at[pl.ds(0, slabs)]
            self.all = pltpu.make_async_remote_copy(
                src_ref=span, dst_ref=span, device_id={"model": at_model[0][1], "cols": q}, **sems
            )
            steps.append(self)

        def land(self):
            self.all.wait_recv()

    def chip(p, t, d, c=0):
        axis = ORDERS[p][t]
        pos = me | {axis: (me[axis] + d) % 4}
        return {"model": pos["x"] * 2 + (core + c) % 2, "cols": pos["z"] * 4 + pos["y"]}

    def spread(t, slabs):
        return Step(slabs, [(piece(p, t, me[ORDERS[p][t]], None, core), chip(p, t, d)) for p in parts for d in (1, 3, 2)])

    def plane(p, d):
        return (me[ORDERS[p][2]] + d) % 4

    def hand_over(pieces, slabs):
        return Step(slabs, [(ref, {"model": at_model[0][1], "cols": q}) for ref in pieces])

    def send_windows(first, last):
        for d in others[first:last]:
            to = away(d)
            pltpu.make_async_remote_copy(
                src_ref=pack.at[to["model"], pl.ds(4 * to["cols"], 6)],
                dst_ref=got.at[mine],
                send_sem=xs_send,
                recv_sem=xs_recv,
                device_id=to,
                device_id_type=MESH,
            ).start()

    mine = ((core * 4 + me["x"]) * 4 + me["z"]) * 4 + me["y"]
    with jax.named_scope("send_first"):
        first = spread(0, 18)
        for pair in range(6):
            got[mine, pair] = pack[m, 4 * q + pair]
        send_windows(0, CUTS[0])
    with jax.named_scope("wait_first"):
        first.land()
    with jax.named_scope("send_second"):
        second = spread(1, 72)
        send_windows(CUTS[0], CUTS[1])
    with jax.named_scope("wait_second"):
        second.land()
    last, passed, lent, lent_on = {}, {}, {}, {}

    def send_plane(n):
        last[n] = Step(96, [(piece(p, 2, plane(p, 0), n, core), chip(p, 2, d)) for p in parts for d in (1, 3)])

    def pass_on(n):
        with jax.named_scope(f"wait_last{n}"):
            last[n].land()
        passed[n] = Step(48, [(piece(p, 2, plane(p, 4 - d), n, core, half=d // 2), chip(p, 2, d)) for p in parts for d in (1, 3)])
        lent[n] = hand_over([piece(p, 2, plane(p, d), n, core) for p in parts for d in (1, 3)], 96)

    def finish(n):
        with jax.named_scope(f"wait_passed{n}"):
            passed[n].land()
        lent_on[n] = hand_over([piece(p, 2, plane(p, 2), n, core) for p in parts], 48)

    with jax.named_scope("send_third"):
        send_plane(0)
        own = hand_over([piece(p, 2, plane(p, 0), None, core) for p in parts], 96)
        send_windows(CUTS[1], 127)
    send_plane(1)
    span = got.at[pl.ds(0, 127)]
    everything = pltpu.make_async_remote_copy(
        src_ref=span, dst_ref=span, send_sem=xs_send, recv_sem=xs_recv, device_id=chip(0, 0, 0, 1), device_id_type=MESH
    )
    with jax.named_scope("wait_windows"):
        everything.wait_recv()
    pass_on(0)
    xs, ys = (x0, x1, x2), (y0, y1, y2)
    with jax.named_scope("turn"):
        for pair in range(6):
            for p in parts:
                rows = []
                for v in range(4):
                    for c in range(2):
                        at = 64 * c
                        if p == 0:
                            rows.append(got[at + 16 * v : at + 16 * v + 16, pair])
                        elif p == 1:
                            rows.append(got[at + v : at + 64 : 4, pair])
                        else:
                            rows += [got[at + 16 * a + 4 * v : at + 16 * a + 4 * v + 4, pair] for a in range(4)]
                rows = jnp.concatenate([r.reshape(-1, LANES) for r in rows], axis=0).T
                for odd in range(2):
                    main = rows[64 * odd : 64 * odd + 64]
                    xs[p][2 * pair + odd, 8 - 4 * p : 72 - 4 * p] = main
                    if p == 1:
                        edge[0, 2 * pair + odd] = main[60:64]
                        edge[1, 2 * pair + odd] = main[0:4]
    halo = []
    for src, dst, d in (
        (x0.at[:, pl.ds(64, 8)], x0.at[:, pl.ds(0, 8)], 1),
        (x2.at[:, pl.ds(0, 8)], x2.at[:, pl.ds(64, 8)], 7),
        (edge.at[0], edge.at[2], 1),
        (edge.at[1], edge.at[3], 7),
    ):
        halo.append(
            pltpu.make_async_remote_copy(
                src_ref=src,
                dst_ref=dst,
                send_sem=halo_send.at[len(halo)],
                recv_sem=halo_recv.at[len(halo)],
                device_id={"model": (m + d) % 8, "cols": q},
                device_id_type=MESH,
            )
        )
        halo[-1].start()

    def conv1(halves, places, spans, groups):
        width = 10 // groups
        tops = [None] * groups
        for p in parts:
            at = [plane(p, d) for d in places]
            lanes = [pl.ds(pl.multiple_of(LANES * v, LANES), LANES) for v in at]
            for dw in range(3):
                right = [[w1g[p, n, v, :, :, :, dw, i].reshape(LANES, LANES) for n in halves for i in range(2)] for v in at]
                right = jnp.concatenate([jnp.concatenate(r, axis=1) for r in right], axis=0)
                for group in range(groups):
                    cols = pl.ds(dw + width * group, width)
                    left = [jnp.concatenate([xs[p][cols, rows, s] for s in lanes], axis=-1) for rows in spans]
                    left = jnp.concatenate(left, axis=1).reshape(-1, 256)
                    term = jnp.dot(left, right, preferred_element_type=F32)
                    tops[group] = term if tops[group] is None else tops[group] + term
        return [top.reshape(width, -1, 256 * len(halves)) for top in tops]

    top_rows, inner, low_rows = pl.ds(0, 8), pl.ds(8, 56), pl.ds(64, 8)

    def near(n):
        with jax.named_scope(f"wait_lent{n}"):
            lent[n].land()
        with jax.named_scope(f"near{n}"):
            for group, top in enumerate(conv1((n,), (3, 1), (inner,), 2)):
                z_acc[n, pl.ds(5 * group, 5), inner] = top

    def rim():
        with jax.named_scope("rim"):
            (top,) = conv1((0, 1), (3, 1), (top_rows, low_rows), 1)
            for n in range(2):
                part = top[:, :, 256 * n : 256 * n + 256]
                z_acc[n, :, top_rows] = part[:, :8]
                z_acc[n, :, low_rows] = part[:, 8:]

    def far(n):
        with jax.named_scope(f"wait_lent_on{n}"):
            lent_on[n].land()
        lanes = slice(256 * n, 256 * n + 256)
        with jax.named_scope(f"far{n}"):
            for group, top in enumerate(conv1((n,), (0, 2), (pl.ds(0, 72),), 2)):
                cols = pl.ds(5 * group, 5)
                act = jnp.maximum(z_acc[n, cols] + top + b1v[:, lanes], 0.0)
                for dh in range(3):
                    ys[dh][cols, :, lanes] = act[:, 4 * dh : 4 * dh + 64].astype(BF16)

        def clear(at_edge, refs, cols, rows):
            @pl.when(at_edge)
            def _():
                for ref in refs:
                    ref[cols, rows, lanes] = jnp.zeros((cols.size, rows.size, 256), BF16)

        clear(q == 0, ys, pl.ds(0, 1), pl.ds(0, 64))
        clear(q == 15, ys, pl.ds(9, 1), pl.ds(0, 64))
        clear(m == 0, (y0,), pl.ds(0, 10), pl.ds(0, 4))
        clear(m == 7, (y2,), pl.ds(0, 10), pl.ds(60, 4))

    def conv2(n):
        lanes = slice(256 * n, 256 * n + 256)
        total = None
        for dh in range(3):
            for dw in range(3):
                tap = 3 * dh + dw
                left = ys[dh][dw : dw + 8, :, lanes].reshape(CHANS, 256)
                right = w2v[CHANS * tap + 256 * n : CHANS * tap + 256 * n + 256, :]
                term = jnp.dot(left, right, preferred_element_type=F32)
                total = term if total is None else total + term
        return total

    pass_on(1)
    near(0)
    near(1)
    finish(0)
    with jax.named_scope("wait_halo"):
        for copy in halo:
            copy.wait_recv()

    @pl.when(m == 0)
    def _():
        x0[:, 0:8] = jnp.zeros((12, 8, CHANS), BF16)
        x1[:, 0:4] = jnp.zeros((12, 4, CHANS), BF16)

    @pl.when(m > 0)
    def _():
        x1[:, 0:4] = edge[2]

    @pl.when(m == 7)
    def _():
        x2[:, 64:72] = jnp.zeros((12, 8, CHANS), BF16)
        x1[:, 68:72] = jnp.zeros((12, 4, CHANS), BF16)

    @pl.when(m < 7)
    def _():
        x1[:, 68:72] = edge[3]

    rim()
    finish(1)
    with jax.named_scope("wait_own_w2"):
        own.land()
        for load in loads[2:]:
            load.wait()
    far(0)
    with jax.named_scope("conv2_0"):
        acc2[...] = conv2(0)
    far(1)
    with jax.named_scope("conv2_1"):
        o_ref[...] = acc2[...] + conv2(1) + b2v[...]

    with jax.named_scope("wait_sends"):
        everything.wait_send()
        for step in steps:
            step.all.wait_send()
        for copy in halo:
            copy.wait_send()


def arrange(sum_ref, o_hbm, turned, sems):
    copies = []
    for g in range(4):
        rows = jnp.transpose(sum_ref[:, 16 * g : 16 * g + 16], (1, 0, 2))
        for h in range(4):
            for image in range(4):
                turned[g, image, h] = rows[4 * h + image]
        copies.append(pltpu.make_async_copy(turned.at[g], o_hbm.at[:, pl.ds(4 * g, 4)], sems.at[g]))
        copies[-1].start()
    for copy in copies:
        copy.wait()


def solution(mesh):
    scratch = [
        pltpu.VMEM((4, LANES, 4, LANES), BF16),
        pltpu.VMEM((9, 4, CHANS), BF16),
        pltpu.VMEM((4616, CHANS), BF16),
        pltpu.VMEM((1, CHANS), F32),
        pltpu.VMEM((1, CHANS), F32),
        pltpu.VMEM((CHANS, CHANS), BF16),
        pltpu.VMEM((8, 66, 4, LANES), BF16),
        pltpu.VMEM((LANES, 6, 4, LANES), BF16),
        *[pltpu.VMEM((12, 72, CHANS), BF16) for _ in range(3)],
        pltpu.VMEM((4, 12, 4, CHANS), BF16),
        pltpu.VMEM((3, 2, 4, 2, 4, 4, 3, 2, 4, LANES), BF16),
        pltpu.VMEM((2, 10, 72, 256), F32),
        *[pltpu.VMEM((10, 64, CHANS), BF16) for _ in range(3)],
        pltpu.VMEM((CHANS, CHANS), F32),
        pltpu.SemaphoreType.DMA((5,)),
        pltpu.SemaphoreType.DMA,
        pltpu.SemaphoreType.DMA,
        pltpu.SemaphoreType.DMA((4,)),
        pltpu.SemaphoreType.DMA((4,)),
        pltpu.SemaphoreType.DMA((11,)),
        pltpu.SemaphoreType.DMA((11,)),
    ]
    vmem = pl.BlockSpec(memory_space=pltpu.VMEM)
    anywhere = pl.BlockSpec(memory_space=pl.ANY)

    def run_local(x_in, w_conv1, b_conv1, w_conv2, b_conv2):
        sums = pl.pallas_call(
            kernel,
            out_shape=jax.ShapeDtypeStruct((CHANS, CHANS), F32),
            in_specs=[anywhere] * 5,
            out_specs=vmem,
            scratch_shapes=scratch,
            compiler_params=pltpu.CompilerParams(collective_id=0, has_side_effects=True, vmem_limit_bytes=VMEM_LIMIT),
            name="two_convs",
        )(
            *(
                pltpu.with_memory_space_constraint(a, pltpu.HBM)
                for a in (
                    x_in.transpose(0, 1, 3, 2),
                    w_conv1.reshape(9, 4, CHANS),
                    w_conv2.reshape(4608, CHANS),
                    b_conv1.reshape(1, CHANS),
                    b_conv2.reshape(1, CHANS),
                )
            )
        )
        return pl.pallas_call(
            arrange,
            out_shape=jax.ShapeDtypeStruct((4, 16, 8, CHANS), F32),
            in_specs=[vmem],
            out_specs=anywhere,
            scratch_shapes=[pltpu.VMEM((4, 4, 4, 8, CHANS), F32), pltpu.SemaphoreType.DMA((4,))],
            compiler_params=pltpu.CompilerParams(vmem_limit_bytes=8 * 2**20),
            name="arrange",
        )(sums.reshape(8, 64, CHANS))

    return jax.shard_map(
        run_local,
        mesh=mesh,
        in_specs=(P("data", None, None, GROUP_AXES), P(None, None, GROUP_AXES, None), P(), P(), P()),
        out_specs=P("data", "model", "cols", None),
        check_vma=False,
    )
```

time: 41.6 us -> 39.6 us (0.952)
  the two profiles are of different devices: /device:TPU:2 before, /device:TPU:1 now
where the time goes in v2:
time: 39.6 us; the launch traced here: 39.5 us
  Pallas kernels  39.5 us (100%)
    pallas_call x1, Pallas kernels, run_local(): pl.pallas_call(kernel, out_shape=jax.ShapeDtypeStruct((CHANS, CHANS), F32...  38.4 us
    pallas_call x1, Pallas kernels, run_local(): pl.pallas_call(arrange, out_shape=jax.ShapeDtypeStruct((4, 16, 8, CHANS),...  1.05 us

profile of v2, /device:TPU:1, one launch (start us, length us, event | category | flops | bytes accessed | tf_op | source)
XLA Modules:
  0.0 39.5 jit_solution(1568916114989832920)
XLA Ops:
  0.0 38.4 %two_convs.1 = f32[512,512]{1,0:T(8,128)S(1)} custom-call(bf16[4,128,4,128]{3,2,1,0:T(4,128)(2,1)} %bitcast.8, bf16[9,4,512]{2,1,0:T(4,128)(2,1)} %bitcast.9, bf16[4608,512]{1,0:T(8,128)(2,1)} %bitcast.7, f32[1,512]{1,0:T(1,128)} %bitcast.10, f32[1,512]{1,0:T(1,128)} %bitcast.11), custom_call_target="tpu_custom_call" | custom-call | tf_op jit(solution)/shard_map/two_convs/pallas_call | solution.py:383
  38.4 1.0 %arrange.1 = f32[4,16,8,512]{3,2,1,0:T(8,128)} custom-call(f32[8,64,512]{2,1,0:T(8,128)S(1)} %bitcast.6), custom_call_target="tpu_custom_call" | custom-call | tf_op jit(solution)/shard_map/arrange/pallas_call | solution.py:403

commit v3 on v2

--- a/solution.py
+++ b/solution.py
@@ -294,8 +294,8 @@
 
     pass_on(1)
     near(0)
+    finish(0)
     near(1)
-    finish(0)
     with jax.named_scope("wait_halo"):
         for copy in halo:
             copy.wait_recv()

time: 39.6 us -> 39.6 us (level)
  no operation moved by 1% of the time
where the time goes in v3:
time: 39.6 us; the launch traced here: 39.5 us
  Pallas kernels  39.5 us (100%)
    pallas_call x1, Pallas kernels, run_local(): pl.pallas_call(kernel, out_shape=jax.ShapeDtypeStruct((CHANS, CHANS), F32...  38.4 us
    pallas_call x1, Pallas kernels, run_local(): pl.pallas_call(arrange, out_shape=jax.ShapeDtypeStruct((4, 16, 8, CHANS),...  1.05 us

profile of v3, /device:TPU:1, one launch (start us, length us, event | category | flops | bytes accessed | tf_op | source)
XLA Modules:
  0.0 39.5 jit_solution(2315323187344217245)
XLA Ops:
  0.0 38.4 %two_convs.1 = f32[512,512]{1,0:T(8,128)S(1)} custom-call(bf16[4,128,4,128]{3,2,1,0:T(4,128)(2,1)} %bitcast.8, bf16[9,4,512]{2,1,0:T(4,128)(2,1)} %bitcast.9, bf16[4608,512]{1,0:T(8,128)(2,1)} %bitcast.7, f32[1,512]{1,0:T(1,128)} %bitcast.10, f32[1,512]{1,0:T(1,128)} %bitcast.11), custom_call_target="tpu_custom_call" | custom-call | tf_op jit(solution)/shard_map/two_convs/pallas_call | solution.py:383
  38.4 1.0 %arrange.1 = f32[4,16,8,512]{3,2,1,0:T(8,128)} custom-call(f32[8,64,512]{2,1,0:T(8,128)S(1)} %bitcast.6), custom_call_target="tpu_custom_call" | custom-call | tf_op jit(solution)/shard_map/arrange/pallas_call | solution.py:403

commit v4 on v2

--- a/solution.py
+++ b/solution.py
@@ -11,7 +11,7 @@
 F32 = jnp.float32
 CHANS = 512
 LANES = 128
-CUTS = (96, 127)
+CUT = 96
 VMEM_LIMIT = 36 * 2**20
 ORDERS = (("y", "z", "x"), ("z", "x", "y"), ("x", "y", "z"))
 
@@ -106,14 +106,18 @@
             k = n_steps[0]
             n_steps[0] += 1
             sems = dict(send_sem=step_send.at[k], recv_sem=step_recv.at[k], device_id_type=MESH)
-            for ref, to in copies:
-                pltpu.make_async_remote_copy(src_ref=ref, dst_ref=ref, device_id=to, **sems).start()
+            self.copies, self.sems = copies, sems
             span = got.at[pl.ds(0, slabs)]
             self.all = pltpu.make_async_remote_copy(
                 src_ref=span, dst_ref=span, device_id={"model": at_model[0][1], "cols": q}, **sems
             )
             steps.append(self)
 
+        def go(self):
+            for ref, to in self.copies:
+                pltpu.make_async_remote_copy(src_ref=ref, dst_ref=ref, device_id=to, **self.sems).start()
+            return self
+
         def land(self):
             self.all.wait_recv()
 
@@ -123,13 +127,13 @@
         return {"model": pos["x"] * 2 + (core + c) % 2, "cols": pos["z"] * 4 + pos["y"]}
 
     def spread(t, slabs):
-        return Step(slabs, [(piece(p, t, me[ORDERS[p][t]], None, core), chip(p, t, d)) for p in parts for d in (1, 3, 2)])
+        return Step(slabs, [(piece(p, t, me[ORDERS[p][t]], None, core), chip(p, t, d)) for p in parts for d in (1, 3, 2)]).go()
 
     def plane(p, d):
         return (me[ORDERS[p][2]] + d) % 4
 
     def hand_over(pieces, slabs):
-        return Step(slabs, [(ref, {"model": at_model[0][1], "cols": q}) for ref in pieces])
+        return Step(slabs, [(ref, {"model": at_model[0][1], "cols": q}) for ref in pieces]).go()
 
     def send_windows(first, last):
         for d in others[first:last]:
@@ -148,12 +152,12 @@
         first = spread(0, 18)
         for pair in range(6):
             got[mine, pair] = pack[m, 4 * q + pair]
-        send_windows(0, CUTS[0])
+        send_windows(0, CUT)
     with jax.named_scope("wait_first"):
         first.land()
     with jax.named_scope("send_second"):
         second = spread(1, 72)
-        send_windows(CUTS[0], CUTS[1])
+        send_windows(CUT, 127)
     with jax.named_scope("wait_second"):
         second.land()
     last, passed, lent, lent_on = {}, {}, {}, {}
@@ -164,7 +168,7 @@
     def pass_on(n):
         with jax.named_scope(f"wait_last{n}"):
             last[n].land()
-        passed[n] = Step(48, [(piece(p, 2, plane(p, 4 - d), n, core, half=d // 2), chip(p, 2, d)) for p in parts for d in (1, 3)])
+        passed[n] = Step(48, [(piece(p, 2, plane(p, 4 - d), n, core, half=d // 2), chip(p, 2, d)) for p in parts for d in (1, 3)]).go()
         lent[n] = hand_over([piece(p, 2, plane(p, d), n, core) for p in parts for d in (1, 3)], 96)
 
     def finish(n):
@@ -173,16 +177,25 @@
         lent_on[n] = hand_over([piece(p, 2, plane(p, 2), n, core) for p in parts], 48)
 
     with jax.named_scope("send_third"):
-        send_plane(0)
+        for n in range(2):
+            send_plane(n)
+        last[0].go()
         own = hand_over([piece(p, 2, plane(p, 0), None, core) for p in parts], 96)
-        send_windows(CUTS[1], 127)
-    send_plane(1)
+    @pl.when(core == 0)
+    def _():
+        last[1].go()
+
     span = got.at[pl.ds(0, 127)]
     everything = pltpu.make_async_remote_copy(
         src_ref=span, dst_ref=span, send_sem=xs_send, recv_sem=xs_recv, device_id=chip(0, 0, 0, 1), device_id_type=MESH
     )
     with jax.named_scope("wait_windows"):
         everything.wait_recv()
+
+    @pl.when(core == 1)
+    def _():
+        last[1].go()
+
     pass_on(0)
     xs, ys = (x0, x1, x2), (y0, y1, y2)
     with jax.named_scope("turn"):

time: 39.6 us -> 40.2 us (1.015)
  no operation moved by 1% of the time
where the time goes in v4:
time: 40.2 us; the launch traced here: 39.7 us
  Pallas kernels  39.7 us (99%)
    pallas_call x1, Pallas kernels, run_local(): pl.pallas_call(kernel, out_shape=jax.ShapeDtypeStruct((CHANS, CHANS), F32...  38.7 us
    pallas_call x1, Pallas kernels, run_local(): pl.pallas_call(arrange, out_shape=jax.ShapeDtypeStruct((4, 16, 8, CHANS),...  1.05 us

profile of v4, /device:TPU:1, one launch (start us, length us, event | category | flops | bytes accessed | tf_op | source)
XLA Modules:
  0.0 39.7 jit_solution(17914580892155080139)
XLA Ops:
  0.0 38.7 %two_convs.1 = f32[512,512]{1,0:T(8,128)S(1)} custom-call(bf16[4,128,4,128]{3,2,1,0:T(4,128)(2,1)} %bitcast.8, bf16[9,4,512]{2,1,0:T(4,128)(2,1)} %bitcast.9, bf16[4608,512]{1,0:T(8,128)(2,1)} %bitcast.7, f32[1,512]{1,0:T(1,128)} %bitcast.10, f32[1,512]{1,0:T(1,128)} %bitcast.11), custom_call_target="tpu_custom_call" | custom-call | tf_op jit(solution)/shard_map/two_convs/pallas_call | solution.py:396
  38.7 1.0 %arrange.1 = f32[4,16,8,512]{3,2,1,0:T(8,128)} custom-call(f32[8,64,512]{2,1,0:T(8,128)S(1)} %bitcast.6), custom_call_target="tpu_custom_call" | custom-call | tf_op jit(solution)/shard_map/arrange/pallas_call | solution.py:416

commit v5 on v4

--- a/solution.py
+++ b/solution.py
@@ -191,12 +191,12 @@
     )
     with jax.named_scope("wait_windows"):
         everything.wait_recv()
+    pass_on(0)
 
     @pl.when(core == 1)
     def _():
         last[1].go()
 
-    pass_on(0)
     xs, ys = (x0, x1, x2), (y0, y1, y2)
     with jax.named_scope("turn"):
         for pair in range(6):

time: 40.2 us -> 41 us (1.020); the launches traced: 39.7 us -> 40.9 us
  Pallas kernels: 39.7 us -> 40.9 us
    pallas_call x1, Pallas kernels: 38.7 us -> 39.9 us  [run_local(): pl.pallas_call(kernel, out_shape=jax.ShapeDtypeStruct((CHANS, CHANS), F32...]
where the time goes in v5:
time: 41 us; the launch traced here: 40.9 us
  Pallas kernels  40.9 us (100%)
    pallas_call x1, Pallas kernels, run_local(): pl.pallas_call(kernel, out_shape=jax.ShapeDtypeStruct((CHANS, CHANS), F32...  39.9 us
    pallas_call x1, Pallas kernels, run_local(): pl.pallas_call(arrange, out_shape=jax.ShapeDtypeStruct((4, 16, 8, CHANS),...  1.05 us

profile of v5, /device:TPU:1, one launch (start us, length us, event | category | flops | bytes accessed | tf_op | source)
XLA Modules:
  0.0 40.9 jit_solution(810437299265564283)
XLA Ops:
  0.0 39.9 %two_convs.1 = f32[512,512]{1,0:T(8,128)S(1)} custom-call(bf16[4,128,4,128]{3,2,1,0:T(4,128)(2,1)} %bitcast.8, bf16[9,4,512]{2,1,0:T(4,128)(2,1)} %bitcast.9, bf16[4608,512]{1,0:T(8,128)(2,1)} %bitcast.7, f32[1,512]{1,0:T(1,128)} %bitcast.10, f32[1,512]{1,0:T(1,128)} %bitcast.11), custom_call_target="tpu_custom_call" | custom-call | tf_op jit(solution)/shard_map/two_convs/pallas_call | solution.py:396
  39.9 1.0 %arrange.1 = f32[4,16,8,512]{3,2,1,0:T(8,128)} custom-call(f32[8,64,512]{2,1,0:T(8,128)S(1)} %bitcast.6), custom_call_target="tpu_custom_call" | custom-call | tf_op jit(solution)/shard_map/arrange/pallas_call | solution.py:416

commit v6 on v5

--- a/solution.py
+++ b/solution.py
@@ -191,7 +191,6 @@
     )
     with jax.named_scope("wait_windows"):
         everything.wait_recv()
-    pass_on(0)
 
     @pl.when(core == 1)
     def _():
@@ -305,6 +304,7 @@
                 total = term if total is None else total + term
         return total
 
+    pass_on(0)
     pass_on(1)
     near(0)
     near(1)

time: 41 us -> 39.7 us (0.968)
  Pallas kernels: 40.9 us -> 39.4 us
    pallas_call x1, Pallas kernels: 39.9 us -> 38.4 us  [run_local(): pl.pallas_call(kernel, out_shape=jax.ShapeDtypeStruct((CHANS, CHANS), F32...]
where the time goes in v6:
time: 39.7 us; the launch traced here: 39.4 us
  Pallas kernels  39.4 us (99%)
    pallas_call x1, Pallas kernels, run_local(): pl.pallas_call(kernel, out_shape=jax.ShapeDtypeStruct((CHANS, CHANS), F32...  38.4 us
    pallas_call x1, Pallas kernels, run_local(): pl.pallas_call(arrange, out_shape=jax.ShapeDtypeStruct((4, 16, 8, CHANS),...  1.05 us

profile of v6, /device:TPU:1, one launch (start us, length us, event | category | flops | bytes accessed | tf_op | source)
XLA Modules:
  0.0 39.4 jit_solution(5326211745728763940)
XLA Ops:
  0.0 38.4 %two_convs.1 = f32[512,512]{1,0:T(8,128)S(1)} custom-call(bf16[4,128,4,128]{3,2,1,0:T(4,128)(2,1)} %bitcast.8, bf16[9,4,512]{2,1,0:T(4,128)(2,1)} %bitcast.9, bf16[4608,512]{1,0:T(8,128)(2,1)} %bitcast.7, f32[1,512]{1,0:T(1,128)} %bitcast.10, f32[1,512]{1,0:T(1,128)} %bitcast.11), custom_call_target="tpu_custom_call" | custom-call | tf_op jit(solution)/shard_map/two_convs/pallas_call | solution.py:396
  38.4 1.0 %arrange.1 = f32[4,16,8,512]{3,2,1,0:T(8,128)} custom-call(f32[8,64,512]{2,1,0:T(8,128)S(1)} %bitcast.6), custom_call_target="tpu_custom_call" | custom-call | tf_op jit(solution)/shard_map/arrange/pallas_call | solution.py:416

commit v7 on v6

--- a/solution.py
+++ b/solution.py
@@ -191,10 +191,6 @@
     )
     with jax.named_scope("wait_windows"):
         everything.wait_recv()
-
-    @pl.when(core == 1)
-    def _():
-        last[1].go()
 
     xs, ys = (x0, x1, x2), (y0, y1, y2)
     with jax.named_scope("turn"):
@@ -304,6 +300,10 @@
                 total = term if total is None else total + term
         return total
 
+    @pl.when(core == 1)
+    def _():
+        last[1].go()
+
     pass_on(0)
     pass_on(1)
     near(0)

time: 39.7 us -> 42.6 us (1.073)
  Pallas kernels: 39.4 us -> 42.4 us
    pallas_call x1, Pallas kernels: 38.4 us -> 41.4 us  [run_local(): pl.pallas_call(kernel, out_shape=jax.ShapeDtypeStruct((CHANS, CHANS), F32...]
where the time goes in v7:
time: 42.6 us; the launch traced here: 42.5 us
  Pallas kernels  42.4 us (100%)
    pallas_call x1, Pallas kernels, run_local(): pl.pallas_call(kernel, out_shape=jax.ShapeDtypeStruct((CHANS, CHANS), F32...  41.4 us
    pallas_call x1, Pallas kernels, run_local(): pl.pallas_call(arrange, out_shape=jax.ShapeDtypeStruct((4, 16, 8, CHANS),...  1.05 us

profile of v7, /device:TPU:1, one launch (start us, length us, event | category | flops | bytes accessed | tf_op | source)
XLA Modules:
  0.0 42.5 jit_solution(15120589248743104330)
XLA Ops:
  0.0 41.4 %two_convs.1 = f32[512,512]{1,0:T(8,128)S(1)} custom-call(bf16[4,128,4,128]{3,2,1,0:T(4,128)(2,1)} %bitcast.8, bf16[9,4,512]{2,1,0:T(4,128)(2,1)} %bitcast.9, bf16[4608,512]{1,0:T(8,128)(2,1)} %bitcast.7, f32[1,512]{1,0:T(1,128)} %bitcast.10, f32[1,512]{1,0:T(1,128)} %bitcast.11), custom_call_target="tpu_custom_call" | custom-call | tf_op jit(solution)/shard_map/two_convs/pallas_call | solution.py:396
  41.4 1.0 %arrange.1 = f32[4,16,8,512]{3,2,1,0:T(8,128)} custom-call(f32[8,64,512]{2,1,0:T(8,128)S(1)} %bitcast.6), custom_call_target="tpu_custom_call" | custom-call | tf_op jit(solution)/shard_map/arrange/pallas_call | solution.py:416

commit v8 on v6

--- a/solution.py
+++ b/solution.py
@@ -305,8 +305,8 @@
         return total
 
     pass_on(0)
+    near(0)
     pass_on(1)
-    near(0)
     near(1)
     finish(0)
     with jax.named_scope("wait_halo"):

time: 39.7 us -> 40.7 us (1.025)
  the two profiles are of different devices: /device:TPU:1 before, /device:TPU:5 now
where the time goes in v8:
time: 40.7 us; the launch traced here: 40.6 us
  Pallas kernels  40.6 us (100%)
    pallas_call x1, Pallas kernels, run_local(): pl.pallas_call(kernel, out_shape=jax.ShapeDtypeStruct((CHANS, CHANS), F32...  39.6 us
    pallas_call x1, Pallas kernels, run_local(): pl.pallas_call(arrange, out_shape=jax.ShapeDtypeStruct((4, 16, 8, CHANS),...  1.05 us

profile of v8, /device:TPU:5, one launch (start us, length us, event | category | flops | bytes accessed | tf_op | source)
XLA Modules:
  0.0 40.6 jit_solution(6766655301116741625)
XLA Ops:
  0.0 39.6 %two_convs.1 = f32[512,512]{1,0:T(8,128)S(1)} custom-call(bf16[4,128,4,128]{3,2,1,0:T(4,128)(2,1)} %bitcast.8, bf16[9,4,512]{2,1,0:T(4,128)(2,1)} %bitcast.9, bf16[4608,512]{1,0:T(8,128)(2,1)} %bitcast.7, f32[1,512]{1,0:T(1,128)} %bitcast.10, f32[1,512]{1,0:T(1,128)} %bitcast.11), custom_call_target="tpu_custom_call" | custom-call | tf_op jit(solution)/shard_map/two_convs/pallas_call | solution.py:396
  39.6 1.0 %arrange.1 = f32[4,16,8,512]{3,2,1,0:T(8,128)} custom-call(f32[8,64,512]{2,1,0:T(8,128)S(1)} %bitcast.6), custom_call_target="tpu_custom_call" | custom-call | tf_op jit(solution)/shard_map/arrange/pallas_call | solution.py:416

commit v9 on v8

--- a/solution.py
+++ b/solution.py
@@ -181,20 +181,13 @@
             send_plane(n)
         last[0].go()
         own = hand_over([piece(p, 2, plane(p, 0), None, core) for p in parts], 96)
-    @pl.when(core == 0)
-    def _():
-        last[1].go()
-
+    last[1].go()
     span = got.at[pl.ds(0, 127)]
     everything = pltpu.make_async_remote_copy(
         src_ref=span, dst_ref=span, send_sem=xs_send, recv_sem=xs_recv, device_id=chip(0, 0, 0, 1), device_id_type=MESH
     )
     with jax.named_scope("wait_windows"):
         everything.wait_recv()
-
-    @pl.when(core == 1)
-    def _():
-        last[1].go()
 
     xs, ys = (x0, x1, x2), (y0, y1, y2)
     with jax.named_scope("turn"):

time: 40.7 us -> 40.7 us (level)
  the two profiles are of different devices: /device:TPU:5 before, /device:TPU:1 now
where the time goes in v9:
time: 40.7 us; the launch traced here: 40.6 us
  Pallas kernels  40.6 us (100%)
    pallas_call x1, Pallas kernels, run_local(): pl.pallas_call(kernel, out_shape=jax.ShapeDtypeStruct((CHANS, CHANS), F32...  39.6 us
    pallas_call x1, Pallas kernels, run_local(): pl.pallas_call(arrange, out_shape=jax.ShapeDtypeStruct((4, 16, 8, CHANS),...  1.05 us

profile of v9, /device:TPU:1, one launch (start us, length us, event | category | flops | bytes accessed | tf_op | source)
XLA Modules:
  0.0 40.6 jit_solution(6619487446546062666)
XLA Ops:
  0.0 39.6 %two_convs.1 = f32[512,512]{1,0:T(8,128)S(1)} custom-call(bf16[4,128,4,128]{3,2,1,0:T(4,128)(2,1)} %bitcast.8, bf16[9,4,512]{2,1,0:T(4,128)(2,1)} %bitcast.9, bf16[4608,512]{1,0:T(8,128)(2,1)} %bitcast.7, f32[1,512]{1,0:T(1,128)} %bitcast.10, f32[1,512]{1,0:T(1,128)} %bitcast.11), custom_call_target="tpu_custom_call" | custom-call | tf_op jit(solution)/shard_map/two_convs/pallas_call | solution.py:389
  39.6 1.0 %arrange.1 = f32[4,16,8,512]{3,2,1,0:T(8,128)} custom-call(f32[8,64,512]{2,1,0:T(8,128)S(1)} %bitcast.6), custom_call_target="tpu_custom_call" | custom-call | tf_op jit(solution)/shard_map/arrange/pallas_call | solution.py:409

commit v10 on v9

--- a/solution.py
+++ b/solution.py
@@ -232,32 +232,41 @@
     def conv1(halves, places, spans, groups):
         width = 10 // groups
         tops = [None] * groups
-        for p in parts:
-            at = [plane(p, d) for d in places]
-            lanes = [pl.ds(pl.multiple_of(LANES * v, LANES), LANES) for v in at]
-            for dw in range(3):
-                right = [[w1g[p, n, v, :, :, :, dw, i].reshape(LANES, LANES) for n in halves for i in range(2)] for v in at]
-                right = jnp.concatenate([jnp.concatenate(r, axis=1) for r in right], axis=0)
-                for group in range(groups):
-                    cols = pl.ds(dw + width * group, width)
-                    left = [jnp.concatenate([xs[p][cols, rows, s] for s in lanes], axis=-1) for rows in spans]
-                    left = jnp.concatenate(left, axis=1).reshape(-1, 256)
-                    term = jnp.dot(left, right, preferred_element_type=F32)
-                    tops[group] = term if tops[group] is None else tops[group] + term
+        taps = [(p, dw, plane(p, d)) for p in parts for dw in range(3) for d in places]
+        for first in range(0, len(taps), 2):
+            two = taps[first : first + 2]
+            right = [[w1g[p, n, v, :, :, :, dw, i].reshape(LANES, LANES) for n in halves for i in range(2)] for p, dw, v in two]
+            right = jnp.concatenate([jnp.concatenate(r, axis=1) for r in right], axis=0)
+            for group in range(groups):
+                left = []
+                for rows in spans:
+                    some = []
+                    for p, dw, v in two:
+                        lanes = pl.ds(pl.multiple_of(LANES * v, LANES), LANES)
+                        some.append(xs[p][pl.ds(dw + width * group, width), rows, lanes])
+                    left.append(jnp.concatenate(some, axis=-1))
+                left = jnp.concatenate(left, axis=1).reshape(-1, LANES * len(two))
+                term = jnp.dot(left, right, preferred_element_type=F32)
+                tops[group] = term if tops[group] is None else tops[group] + term
         return [top.reshape(width, -1, 256 * len(halves)) for top in tops]
 
     top_rows, inner, low_rows = pl.ds(0, 8), pl.ds(8, 56), pl.ds(64, 8)
+
+    def here(n):
+        with jax.named_scope(f"here{n}"):
+            for group, top in enumerate(conv1((n,), (0,), (inner,), 2)):
+                z_acc[n, pl.ds(5 * group, 5), inner] = top
 
     def near(n):
         with jax.named_scope(f"wait_lent{n}"):
             lent[n].land()
         with jax.named_scope(f"near{n}"):
             for group, top in enumerate(conv1((n,), (3, 1), (inner,), 2)):
-                z_acc[n, pl.ds(5 * group, 5), inner] = top
+                z_acc[n, pl.ds(5 * group, 5), inner] += top
 
     def rim():
         with jax.named_scope("rim"):
-            (top,) = conv1((0, 1), (3, 1), (top_rows, low_rows), 1)
+            (top,) = conv1((0, 1), (0, 3, 1), (top_rows, low_rows), 1)
             for n in range(2):
                 part = top[:, :, 256 * n : 256 * n + 256]
                 z_acc[n, :, top_rows] = part[:, :8]
@@ -268,7 +277,7 @@
             lent_on[n].land()
         lanes = slice(256 * n, 256 * n + 256)
         with jax.named_scope(f"far{n}"):
-            for group, top in enumerate(conv1((n,), (0, 2), (pl.ds(0, 72),), 2)):
+            for group, top in enumerate(conv1((n,), (2,), (pl.ds(0, 72),), 2)):
                 cols = pl.ds(5 * group, 5)
                 act = jnp.maximum(z_acc[n, cols] + top + b1v[:, lanes], 0.0)
                 for dh in range(3):
@@ -298,8 +307,12 @@
         return total
 
     pass_on(0)
+    with jax.named_scope("wait_own"):
+        own.land()
+    here(0)
+    here(1)
+    pass_on(1)
     near(0)
-    pass_on(1)
     near(1)
     finish(0)
     with jax.named_scope("wait_halo"):
@@ -326,8 +339,7 @@
 
     rim()
     finish(1)
-    with jax.named_scope("wait_own_w2"):
-        own.land()
+    with jax.named_scope("wait_w2"):
         for load in loads[2:]:
             load.wait()
     far(0)

time: 40.7 us -> 38.7 us (0.951)
  Pallas kernels: 40.6 us -> 38.6 us
    pallas_call x1, Pallas kernels: 39.6 us -> 37.6 us  [run_local(): pl.pallas_call(kernel, out_shape=jax.ShapeDtypeStruct((CHANS, CHANS), F32...]
where the time goes in v10:
time: 38.7 us; the launch traced here: 38.6 us
  Pallas kernels  38.6 us (100%)
    pallas_call x1, Pallas kernels, run_local(): pl.pallas_call(kernel, out_shape=jax.ShapeDtypeStruct((CHANS, CHANS), F32...  37.6 us
    pallas_call x1, Pallas kernels, run_local(): pl.pallas_call(arrange, out_shape=jax.ShapeDtypeStruct((4, 16, 8, CHANS),...  1.05 us

profile of v10, /device:TPU:1, one launch (start us, length us, event | category | flops | bytes accessed | tf_op | source)
XLA Modules:
  0.0 38.6 jit_solution(11390394237669561290)
XLA Ops:
  0.0 37.6 %two_convs.1 = f32[512,512]{1,0:T(8,128)S(1)} custom-call(bf16[4,128,4,128]{3,2,1,0:T(4,128)(2,1)} %bitcast.8, bf16[9,4,512]{2,1,0:T(4,128)(2,1)} %bitcast.9, bf16[4608,512]{1,0:T(8,128)(2,1)} %bitcast.7, f32[1,512]{1,0:T(1,128)} %bitcast.10, f32[1,512]{1,0:T(1,128)} %bitcast.11), custom_call_target="tpu_custom_call" | custom-call | tf_op jit(solution)/shard_map/two_convs/pallas_call | solution.py:401
  37.6 1.0 %arrange.1 = f32[4,16,8,512]{3,2,1,0:T(8,128)} custom-call(f32[8,64,512]{2,1,0:T(8,128)S(1)} %bitcast.6), custom_call_target="tpu_custom_call" | custom-call | tf_op jit(solution)/shard_map/arrange/pallas_call | solution.py:421

commit v11 on v10

--- a/solution.py
+++ b/solution.py
@@ -306,10 +306,10 @@
                 total = term if total is None else total + term
         return total
 
-    pass_on(0)
     with jax.named_scope("wait_own"):
         own.land()
     here(0)
+    pass_on(0)
     here(1)
     pass_on(1)
     near(0)

time: 38.7 us -> 38.7 us (level)
  no operation moved by 1% of the time
where the time goes in v11:
time: 38.7 us; the launch traced here: 38.6 us
  Pallas kernels  38.6 us (100%)
    pallas_call x1, Pallas kernels, run_local(): pl.pallas_call(kernel, out_shape=jax.ShapeDtypeStruct((CHANS, CHANS), F32...  37.6 us
    pallas_call x1, Pallas kernels, run_local(): pl.pallas_call(arrange, out_shape=jax.ShapeDtypeStruct((4, 16, 8, CHANS),...  1.05 us

profile of v11, /device:TPU:1, one launch (start us, length us, event | category | flops | bytes accessed | tf_op | source)
XLA Modules:
  0.0 38.6 jit_solution(5078906478732334433)
XLA Ops:
  0.0 37.6 %two_convs.1 = f32[512,512]{1,0:T(8,128)S(1)} custom-call(bf16[4,128,4,128]{3,2,1,0:T(4,128)(2,1)} %bitcast.8, bf16[9,4,512]{2,1,0:T(4,128)(2,1)} %bitcast.9, bf16[4608,512]{1,0:T(8,128)(2,1)} %bitcast.7, f32[1,512]{1,0:T(1,128)} %bitcast.10, f32[1,512]{1,0:T(1,128)} %bitcast.11), custom_call_target="tpu_custom_call" | custom-call | tf_op jit(solution)/shard_map/two_convs/pallas_call | solution.py:401
  37.6 1.0 %arrange.1 = f32[4,16,8,512]{3,2,1,0:T(8,128)} custom-call(f32[8,64,512]{2,1,0:T(8,128)S(1)} %bitcast.6), custom_call_target="tpu_custom_call" | custom-call | tf_op jit(solution)/shard_map/arrange/pallas_call | solution.py:421

commit v12 on v10

--- a/solution.py
+++ b/solution.py
@@ -179,15 +179,25 @@
     with jax.named_scope("send_third"):
         for n in range(2):
             send_plane(n)
+        own = hand_over([piece(p, 2, plane(p, 0), None, core) for p in parts], 96)
+
+    @pl.when(core == 0)
+    def _():
         last[0].go()
-        own = hand_over([piece(p, 2, plane(p, 0), None, core) for p in parts], 96)
-    last[1].go()
+        last[1].go()
+
     span = got.at[pl.ds(0, 127)]
     everything = pltpu.make_async_remote_copy(
         src_ref=span, dst_ref=span, send_sem=xs_send, recv_sem=xs_recv, device_id=chip(0, 0, 0, 1), device_id_type=MESH
     )
     with jax.named_scope("wait_windows"):
         everything.wait_recv()
+
+    @pl.when(core == 1)
+    def _():
+        last[0].go()
+        last[1].go()
+
 
     xs, ys = (x0, x1, x2), (y0, y1, y2)
     with jax.named_scope("turn"):

time: 38.7 us -> 40.1 us (1.036)
  Pallas kernels: 38.6 us -> 39.9 us
    pallas_call x1, Pallas kernels: 37.6 us -> 38.9 us  [run_local(): pl.pallas_call(kernel, out_shape=jax.ShapeDtypeStruct((CHANS, CHANS), F32...]
where the time goes in v12:
time: 40.1 us; the launch traced here: 39.9 us
  Pallas kernels  39.9 us (100%)
    pallas_call x1, Pallas kernels, run_local(): pl.pallas_call(kernel, out_shape=jax.ShapeDtypeStruct((CHANS, CHANS), F32...  38.9 us
    pallas_call x1, Pallas kernels, run_local(): pl.pallas_call(arrange, out_shape=jax.ShapeDtypeStruct((4, 16, 8, CHANS),...  1.05 us

profile of v12, /device:TPU:1, one launch (start us, length us, event | category | flops | bytes accessed | tf_op | source)
XLA Modules:
  0.0 39.9 jit_solution(3522638539366629861)
XLA Ops:
  0.0 38.9 %two_convs.1 = f32[512,512]{1,0:T(8,128)S(1)} custom-call(bf16[4,128,4,128]{3,2,1,0:T(4,128)(2,1)} %bitcast.8, bf16[9,4,512]{2,1,0:T(4,128)(2,1)} %bitcast.9, bf16[4608,512]{1,0:T(8,128)(2,1)} %bitcast.7, f32[1,512]{1,0:T(1,128)} %bitcast.10, f32[1,512]{1,0:T(1,128)} %bitcast.11), custom_call_target="tpu_custom_call" | custom-call | tf_op jit(solution)/shard_map/two_convs/pallas_call | solution.py:411
  38.9 1.0 %arrange.1 = f32[4,16,8,512]{3,2,1,0:T(8,128)} custom-call(f32[8,64,512]{2,1,0:T(8,128)S(1)} %bitcast.6), custom_call_target="tpu_custom_call" | custom-call | tf_op jit(solution)/shard_map/arrange/pallas_call | solution.py:431

commit v13 on v12

--- a/solution.py
+++ b/solution.py
@@ -179,11 +179,11 @@
     with jax.named_scope("send_third"):
         for n in range(2):
             send_plane(n)
+        last[0].go()
         own = hand_over([piece(p, 2, plane(p, 0), None, core) for p in parts], 96)
 
     @pl.when(core == 0)
     def _():
-        last[0].go()
         last[1].go()
 
     span = got.at[pl.ds(0, 127)]
@@ -195,7 +195,6 @@
 
     @pl.when(core == 1)
     def _():
-        last[0].go()
         last[1].go()
 
 

time: 40.1 us -> 38.9 us (0.970)
  Pallas kernels: 39.9 us -> 38.7 us
    pallas_call x1, Pallas kernels: 38.9 us -> 37.6 us  [run_local(): pl.pallas_call(kernel, out_shape=jax.ShapeDtypeStruct((CHANS, CHANS), F32...]
where the time goes in v13:
time: 38.9 us; the launch traced here: 38.7 us
  Pallas kernels  38.7 us (99%)
    pallas_call x1, Pallas kernels, run_local(): pl.pallas_call(kernel, out_shape=jax.ShapeDtypeStruct((CHANS, CHANS), F32...  37.6 us
    pallas_call x1, Pallas kernels, run_local(): pl.pallas_call(arrange, out_shape=jax.ShapeDtypeStruct((4, 16, 8, CHANS),...  1.05 us

profile of v13, /device:TPU:1, one launch (start us, length us, event | category | flops | bytes accessed | tf_op | source)
XLA Modules:
  0.0 38.7 jit_solution(10264582652983630282)
XLA Ops:
  0.0 37.6 %two_convs.1 = f32[512,512]{1,0:T(8,128)S(1)} custom-call(bf16[4,128,4,128]{3,2,1,0:T(4,128)(2,1)} %bitcast.8, bf16[9,4,512]{2,1,0:T(4,128)(2,1)} %bitcast.9, bf16[4608,512]{1,0:T(8,128)(2,1)} %bitcast.7, f32[1,512]{1,0:T(1,128)} %bitcast.10, f32[1,512]{1,0:T(1,128)} %bitcast.11), custom_call_target="tpu_custom_call" | custom-call | tf_op jit(solution)/shard_map/two_convs/pallas_call | solution.py:410
  37.6 1.0 %arrange.1 = f32[4,16,8,512]{3,2,1,0:T(8,128)} custom-call(f32[8,64,512]{2,1,0:T(8,128)S(1)} %bitcast.6), custom_call_target="tpu_custom_call" | custom-call | tf_op jit(solution)/shard_map/arrange/pallas_call | solution.py:430

commit v14 on v10

--- a/solution.py
+++ b/solution.py
@@ -53,7 +53,6 @@
     me = {"x": m // 2, "z": q // 4, "y": q % 4}
     core = m % 2
     parts = range(3)
-    barrier = pltpu.get_barrier_semaphore()
 
     at_model = [[(me["x"] + dx) % 4 * 2 + (core + dk) % 2 for dk in range(2)] for dx in range(4)]
     at_cols = [[(me["z"] + dz) % 4 * 4 + (me["y"] + dy) % 4 for dy in range(4)] for dz in range(4)]
@@ -71,10 +70,6 @@
     ]
     for load in loads:
         load.start()
-    with jax.named_scope("announce"):
-        for d in sorted(others, key=lambda d: -sum(min(o, 4 - o) for o in d[:3])):
-            pl.semaphore_signal(barrier, inc=1, device_id=away(d), device_id_type=MESH)
-
     def piece(p, t, v, n, c, place=None, half=None):
         done = ORDERS[p][:t]
         rest = [a for a in "xzy" if a != ORDERS[p][2]]
@@ -95,8 +90,6 @@
         loads[0].wait()
     with jax.named_scope("pack"):
         pack_windows(xv, a_scr, pack)
-    with jax.named_scope("wait_barrier"):
-        pl.semaphore_wait(barrier, 127)
 
     n_steps = [0]
     steps = []
@@ -404,7 +397,7 @@
             in_specs=[anywhere] * 5,
             out_specs=vmem,
             scratch_shapes=scratch,
-            compiler_params=pltpu.CompilerParams(collective_id=0, has_side_effects=True, vmem_limit_bytes=VMEM_LIMIT),
+            compiler_params=pltpu.CompilerParams(has_side_effects=True, vmem_limit_bytes=VMEM_LIMIT),
             name="two_convs",
         )(
             *(

time: 38.7 us -> 45.8 us (1.18)
  Pallas kernels: 38.6 us -> 45.7 us
    pallas_call x1, Pallas kernels: 37.6 us -> 44.7 us  [run_local(): pl.pallas_call(kernel, out_shape=jax.ShapeDtypeStruct((CHANS, CHANS), F32...]
where the time goes in v14:
time: 45.8 us; the launch traced here: 45.7 us
  Pallas kernels  45.7 us (100%)
    pallas_call x1, Pallas kernels, run_local(): pl.pallas_call(kernel, out_shape=jax.ShapeDtypeStruct((CHANS, CHANS), F32...  44.7 us
    pallas_call x1, Pallas kernels, run_local(): pl.pallas_call(arrange, out_shape=jax.ShapeDtypeStruct((4, 16, 8, CHANS),...  1.05 us

profile of v14, /device:TPU:1, one launch (start us, length us, event | category | flops | bytes accessed | tf_op | source)
XLA Modules:
  0.0 45.7 jit_solution(14997447574931200915)
XLA Ops:
  0.0 44.7 %two_convs.1 = f32[512,512]{1,0:T(8,128)S(1)} custom-call(bf16[4,128,4,128]{3,2,1,0:T(4,128)(2,1)} %bitcast.8, bf16[9,4,512]{2,1,0:T(4,128)(2,1)} %bitcast.9, bf16[4608,512]{1,0:T(8,128)(2,1)} %bitcast.7, f32[1,512]{1,0:T(1,128)} %bitcast.10, f32[1,512]{1,0:T(1,128)} %bitcast.11), custom_call_target="tpu_custom_call" | custom-call | tf_op jit(solution)/shard_map/two_convs/pallas_call | solution.py:394
  44.7 1.0 %arrange.1 = f32[4,16,8,512]{3,2,1,0:T(8,128)} custom-call(f32[8,64,512]{2,1,0:T(8,128)S(1)} %bitcast.6), custom_call_target="tpu_custom_call" | custom-call | tf_op jit(solution)/shard_map/arrange/pallas_call | solution.py:414

commit v15 on v13

--- a/solution.py
+++ b/solution.py
@@ -169,6 +169,12 @@
         with jax.named_scope(f"wait_last{n}"):
             last[n].land()
         passed[n] = Step(48, [(piece(p, 2, plane(p, 4 - d), n, core, half=d // 2), chip(p, 2, d)) for p in parts for d in (1, 3)]).go()
+        if n == 0:
+
+            @pl.when(core == 1)
+            def _():
+                last[1].go()
+
         lent[n] = hand_over([piece(p, 2, plane(p, d), n, core) for p in parts for d in (1, 3)], 96)
 
     def finish(n):
@@ -192,11 +198,6 @@
     )
     with jax.named_scope("wait_windows"):
         everything.wait_recv()
-
-    @pl.when(core == 1)
-    def _():
-        last[1].go()
-
 
     xs, ys = (x0, x1, x2), (y0, y1, y2)
     with jax.named_scope("turn"):
@@ -320,8 +321,8 @@
         own.land()
     here(0)
     here(1)
+    near(0)
     pass_on(1)
-    near(0)
     near(1)
     finish(0)
     with jax.named_scope("wait_halo"):

time: 38.9 us -> 42.3 us (1.087)
  Pallas kernels: 38.7 us -> 42.2 us
    pallas_call x1, Pallas kernels: 37.6 us -> 41.2 us  [run_local(): pl.pallas_call(kernel, out_shape=jax.ShapeDtypeStruct((CHANS, CHANS), F32...]
where the time goes in v15:
time: 42.3 us; the launch traced here: 42.2 us
  Pallas kernels  42.2 us (100%)
    pallas_call x1, Pallas kernels, run_local(): pl.pallas_call(kernel, out_shape=jax.ShapeDtypeStruct((CHANS, CHANS), F32...  41.2 us
    pallas_call x1, Pallas kernels, run_local(): pl.pallas_call(arrange, out_shape=jax.ShapeDtypeStruct((4, 16, 8, CHANS),...  1.05 us

profile of v15, /device:TPU:1, one launch (start us, length us, event | category | flops | bytes accessed | tf_op | source)
XLA Modules:
  0.0 42.2 jit_solution(245713998360614698)
XLA Ops:
  0.0 41.2 %two_convs.1 = f32[512,512]{1,0:T(8,128)S(1)} custom-call(bf16[4,128,4,128]{3,2,1,0:T(4,128)(2,1)} %bitcast.8, bf16[9,4,512]{2,1,0:T(4,128)(2,1)} %bitcast.9, bf16[4608,512]{1,0:T(8,128)(2,1)} %bitcast.7, f32[1,512]{1,0:T(1,128)} %bitcast.10, f32[1,512]{1,0:T(1,128)} %bitcast.11), custom_call_target="tpu_custom_call" | custom-call | tf_op jit(solution)/shard_map/two_convs/pallas_call | solution.py:411
  41.2 1.0 %arrange.1 = f32[4,16,8,512]{3,2,1,0:T(8,128)} custom-call(f32[8,64,512]{2,1,0:T(8,128)S(1)} %bitcast.6), custom_call_target="tpu_custom_call" | custom-call | tf_op jit(solution)/shard_map/arrange/pallas_call | solution.py:431

commit v16 on v15

--- a/solution.py
+++ b/solution.py
@@ -321,8 +321,8 @@
         own.land()
     here(0)
     here(1)
+    pass_on(1)
     near(0)
-    pass_on(1)
     near(1)
     finish(0)
     with jax.named_scope("wait_halo"):

time: 42.3 us -> 42.1 us (level)
  no operation moved by 1% of the time
where the time goes in v16:
time: 42.1 us; the launch traced here: 42 us
  Pallas kernels  42 us (100%)
    pallas_call x1, Pallas kernels, run_local(): pl.pallas_call(kernel, out_shape=jax.ShapeDtypeStruct((CHANS, CHANS), F32...  41 us
    pallas_call x1, Pallas kernels, run_local(): pl.pallas_call(arrange, out_shape=jax.ShapeDtypeStruct((4, 16, 8, CHANS),...  1.05 us

profile of v16, /device:TPU:1, one launch (start us, length us, event | category | flops | bytes accessed | tf_op | source)
XLA Modules:
  0.0 42.0 jit_solution(2835214396446263590)
XLA Ops:
  0.0 41.0 %two_convs.1 = f32[512,512]{1,0:T(8,128)S(1)} custom-call(bf16[4,128,4,128]{3,2,1,0:T(4,128)(2,1)} %bitcast.8, bf16[9,4,512]{2,1,0:T(4,128)(2,1)} %bitcast.9, bf16[4608,512]{1,0:T(8,128)(2,1)} %bitcast.7, f32[1,512]{1,0:T(1,128)} %bitcast.10, f32[1,512]{1,0:T(1,128)} %bitcast.11), custom_call_target="tpu_custom_call" | custom-call | tf_op jit(solution)/shard_map/two_convs/pallas_call | solution.py:411
  41.0 1.0 %arrange.1 = f32[4,16,8,512]{3,2,1,0:T(8,128)} custom-call(f32[8,64,512]{2,1,0:T(8,128)S(1)} %bitcast.6), custom_call_target="tpu_custom_call" | custom-call | tf_op jit(solution)/shard_map/arrange/pallas_call | solution.py:431

commit v17 on v10

--- a/solution.py
+++ b/solution.py
@@ -210,25 +210,6 @@
                     if p == 1:
                         edge[0, 2 * pair + odd] = main[60:64]
                         edge[1, 2 * pair + odd] = main[0:4]
-    halo = []
-    for src, dst, d in (
-        (x0.at[:, pl.ds(64, 8)], x0.at[:, pl.ds(0, 8)], 1),
-        (x2.at[:, pl.ds(0, 8)], x2.at[:, pl.ds(64, 8)], 7),
-        (edge.at[0], edge.at[2], 1),
-        (edge.at[1], edge.at[3], 7),
-    ):
-        halo.append(
-            pltpu.make_async_remote_copy(
-                src_ref=src,
-                dst_ref=dst,
-                send_sem=halo_send.at[len(halo)],
-                recv_sem=halo_recv.at[len(halo)],
-                device_id={"model": (m + d) % 8, "cols": q},
-                device_id_type=MESH,
-            )
-        )
-        halo[-1].start()
-
     def conv1(halves, places, spans, groups):
         width = 10 // groups
         tops = [None] * groups
@@ -307,6 +288,24 @@
         return total
 
     pass_on(0)
+    halo = []
+    for src, dst, d in (
+        (x0.at[:, pl.ds(64, 8)], x0.at[:, pl.ds(0, 8)], 1),
+        (x2.at[:, pl.ds(0, 8)], x2.at[:, pl.ds(64, 8)], 7),
+        (edge.at[0], edge.at[2], 1),
+        (edge.at[1], edge.at[3], 7),
+    ):
+        halo.append(
+            pltpu.make_async_remote_copy(
+                src_ref=src,
+                dst_ref=dst,
+                send_sem=halo_send.at[len(halo)],
+                recv_sem=halo_recv.at[len(halo)],
+                device_id={"model": (m + d) % 8, "cols": q},
+                device_id_type=MESH,
+            )
+        )
+        halo[-1].start()
     with jax.named_scope("wait_own"):
         own.land()
     here(0)

time: 38.7 us -> 38.8 us (level)
  no operation moved by 1% of the time
where the time goes in v17:
time: 38.8 us; the launch traced here: 38.7 us
  Pallas kernels  38.7 us (100%)
    pallas_call x1, Pallas kernels, run_local(): pl.pallas_call(kernel, out_shape=jax.ShapeDtypeStruct((CHANS, CHANS), F32...  37.7 us
    pallas_call x1, Pallas kernels, run_local(): pl.pallas_call(arrange, out_shape=jax.ShapeDtypeStruct((4, 16, 8, CHANS),...  1.05 us

profile of v17, /device:TPU:1, one launch (start us, length us, event | category | flops | bytes accessed | tf_op | source)
XLA Modules:
  0.0 38.7 jit_solution(12142861879591914120)
XLA Ops:
  0.0 37.7 %two_convs.1 = f32[512,512]{1,0:T(8,128)S(1)} custom-call(bf16[4,128,4,128]{3,2,1,0:T(4,128)(2,1)} %bitcast.8, bf16[9,4,512]{2,1,0:T(4,128)(2,1)} %bitcast.9, bf16[4608,512]{1,0:T(8,128)(2,1)} %bitcast.7, f32[1,512]{1,0:T(1,128)} %bitcast.10, f32[1,512]{1,0:T(1,128)} %bitcast.11), custom_call_target="tpu_custom_call" | custom-call | tf_op jit(solution)/shard_map/two_convs/pallas_call | solution.py:400
  37.7 1.0 %arrange.1 = f32[4,16,8,512]{3,2,1,0:T(8,128)} custom-call(f32[8,64,512]{2,1,0:T(8,128)S(1)} %bitcast.6), custom_call_target="tpu_custom_call" | custom-call | tf_op jit(solution)/shard_map/arrange/pallas_call | solution.py:420

commit v18 on v17

--- a/solution.py
+++ b/solution.py
@@ -288,6 +288,11 @@
         return total
 
     pass_on(0)
+    with jax.named_scope("wait_own"):
+        own.land()
+    here(0)
+    here(1)
+    pass_on(1)
     halo = []
     for src, dst, d in (
         (x0.at[:, pl.ds(64, 8)], x0.at[:, pl.ds(0, 8)], 1),
@@ -306,11 +311,6 @@
             )
         )
         halo[-1].start()
-    with jax.named_scope("wait_own"):
-        own.land()
-    here(0)
-    here(1)
-    pass_on(1)
     near(0)
     near(1)
     finish(0)

time: 38.8 us -> 40.2 us (1.036)
  Pallas kernels: 38.7 us -> 40.1 us
    pallas_call x1, Pallas kernels: 37.7 us -> 39 us  [run_local(): pl.pallas_call(kernel, out_shape=jax.ShapeDtypeStruct((CHANS, CHANS), F32...]
where the time goes in v18:
time: 40.2 us; the launch traced here: 40.1 us
  Pallas kernels  40.1 us (100%)
    pallas_call x1, Pallas kernels, run_local(): pl.pallas_call(kernel, out_shape=jax.ShapeDtypeStruct((CHANS, CHANS), F32...  39 us
    pallas_call x1, Pallas kernels, run_local(): pl.pallas_call(arrange, out_shape=jax.ShapeDtypeStruct((4, 16, 8, CHANS),...  1.05 us

profile of v18, /device:TPU:1, one launch (start us, length us, event | category | flops | bytes accessed | tf_op | source)
XLA Modules:
  0.0 40.1 jit_solution(18006348544968843505)
XLA Ops:
  0.0 39.0 %two_convs.1 = f32[512,512]{1,0:T(8,128)S(1)} custom-call(bf16[4,128,4,128]{3,2,1,0:T(4,128)(2,1)} %bitcast.8, bf16[9,4,512]{2,1,0:T(4,128)(2,1)} %bitcast.9, bf16[4608,512]{1,0:T(8,128)(2,1)} %bitcast.7, f32[1,512]{1,0:T(1,128)} %bitcast.10, f32[1,512]{1,0:T(1,128)} %bitcast.11), custom_call_target="tpu_custom_call" | custom-call | tf_op jit(solution)/shard_map/two_convs/pallas_call | solution.py:400
  39.0 1.0 %arrange.1 = f32[4,16,8,512]{3,2,1,0:T(8,128)} custom-call(f32[8,64,512]{2,1,0:T(8,128)S(1)} %bitcast.6), custom_call_target="tpu_custom_call" | custom-call | tf_op jit(solution)/shard_map/arrange/pallas_call | solution.py:420

commit v19 on v10

--- a/solution.py
+++ b/solution.py
@@ -11,7 +11,7 @@
 F32 = jnp.float32
 CHANS = 512
 LANES = 128
-CUT = 96
+CUT = 104
 VMEM_LIMIT = 36 * 2**20
 ORDERS = (("y", "z", "x"), ("z", "x", "y"), ("x", "y", "z"))
 

time: 38.7 us -> 40.6 us (1.049)
  Pallas kernels: 38.6 us -> 40.5 us
    pallas_call x1, Pallas kernels: 37.6 us -> 39.4 us  [run_local(): pl.pallas_call(kernel, out_shape=jax.ShapeDtypeStruct((CHANS, CHANS), F32...]
where the time goes in v19:
time: 40.6 us; the launch traced here: 40.5 us
  Pallas kernels  40.5 us (100%)
    pallas_call x1, Pallas kernels, run_local(): pl.pallas_call(kernel, out_shape=jax.ShapeDtypeStruct((CHANS, CHANS), F32...  39.4 us
    pallas_call x1, Pallas kernels, run_local(): pl.pallas_call(arrange, out_shape=jax.ShapeDtypeStruct((4, 16, 8, CHANS),...  1.05 us

profile of v19, /device:TPU:1, one launch (start us, length us, event | category | flops | bytes accessed | tf_op | source)
XLA Modules:
  0.0 40.5 jit_solution(10182534287361085824)
XLA Ops:
  0.0 39.4 %two_convs.1 = f32[512,512]{1,0:T(8,128)S(1)} custom-call(bf16[4,128,4,128]{3,2,1,0:T(4,128)(2,1)} %bitcast.8, bf16[9,4,512]{2,1,0:T(4,128)(2,1)} %bitcast.9, bf16[4608,512]{1,0:T(8,128)(2,1)} %bitcast.7, f32[1,512]{1,0:T(1,128)} %bitcast.10, f32[1,512]{1,0:T(1,128)} %bitcast.11), custom_call_target="tpu_custom_call" | custom-call | tf_op jit(solution)/shard_map/two_convs/pallas_call | solution.py:401
  39.5 1.0 %arrange.1 = f32[4,16,8,512]{3,2,1,0:T(8,128)} custom-call(f32[8,64,512]{2,1,0:T(8,128)S(1)} %bitcast.6), custom_call_target="tpu_custom_call" | custom-call | tf_op jit(solution)/shard_map/arrange/pallas_call | solution.py:421

commit v20 on v19

--- a/solution.py
+++ b/solution.py
@@ -11,7 +11,7 @@
 F32 = jnp.float32
 CHANS = 512
 LANES = 128
-CUT = 104
+CUT = 88
 VMEM_LIMIT = 36 * 2**20
 ORDERS = (("y", "z", "x"), ("z", "x", "y"), ("x", "y", "z"))
 

time: 40.6 us -> 39.2 us (0.966)
  Pallas kernels: 40.5 us -> 39.1 us
    pallas_call x1, Pallas kernels: 39.4 us -> 38 us  [run_local(): pl.pallas_call(kernel, out_shape=jax.ShapeDtypeStruct((CHANS, CHANS), F32...]
where the time goes in v20:
time: 39.2 us; the launch traced here: 39.1 us
  Pallas kernels  39.1 us (100%)
    pallas_call x1, Pallas kernels, run_local(): pl.pallas_call(kernel, out_shape=jax.ShapeDtypeStruct((CHANS, CHANS), F32...  38 us
    pallas_call x1, Pallas kernels, run_local(): pl.pallas_call(arrange, out_shape=jax.ShapeDtypeStruct((4, 16, 8, CHANS),...  1.05 us

profile of v20, /device:TPU:1, one launch (start us, length us, event | category | flops | bytes accessed | tf_op | source)
XLA Modules:
  0.0 39.1 jit_solution(3182275014990096221)
XLA Ops:
  0.0 38.0 %two_convs.1 = f32[512,512]{1,0:T(8,128)S(1)} custom-call(bf16[4,128,4,128]{3,2,1,0:T(4,128)(2,1)} %bitcast.8, bf16[9,4,512]{2,1,0:T(4,128)(2,1)} %bitcast.9, bf16[4608,512]{1,0:T(8,128)(2,1)} %bitcast.7, f32[1,512]{1,0:T(1,128)} %bitcast.10, f32[1,512]{1,0:T(1,128)} %bitcast.11), custom_call_target="tpu_custom_call" | custom-call | tf_op jit(solution)/shard_map/two_convs/pallas_call | solution.py:401
  38.0 1.0 %arrange.1 = f32[4,16,8,512]{3,2,1,0:T(8,128)} custom-call(f32[8,64,512]{2,1,0:T(8,128)S(1)} %bitcast.6), custom_call_target="tpu_custom_call" | custom-call | tf_op jit(solution)/shard_map/arrange/pallas_call | solution.py:421

commit v21 on v10

--- a/solution.py
+++ b/solution.py
@@ -13,7 +13,7 @@
 LANES = 128
 CUT = 96
 VMEM_LIMIT = 36 * 2**20
-ORDERS = (("y", "z", "x"), ("z", "x", "y"), ("x", "y", "z"))
+ORDERS = (("z", "y", "x"), ("x", "z", "y"), ("x", "y", "z"))
 
 
 def one_hot(shape, col_of_row):

time: 38.7 us -> 41.9 us (1.083)
  Pallas kernels: 38.6 us -> 41.8 us
    pallas_call x1, Pallas kernels: 37.6 us -> 40.7 us  [run_local(): pl.pallas_call(kernel, out_shape=jax.ShapeDtypeStruct((CHANS, CHANS), F32...]
where the time goes in v21:
time: 41.9 us; the launch traced here: 41.8 us
  Pallas kernels  41.8 us (100%)
    pallas_call x1, Pallas kernels, run_local(): pl.pallas_call(kernel, out_shape=jax.ShapeDtypeStruct((CHANS, CHANS), F32...  40.7 us
    pallas_call x1, Pallas kernels, run_local(): pl.pallas_call(arrange, out_shape=jax.ShapeDtypeStruct((4, 16, 8, CHANS),...  1.05 us

profile of v21, /device:TPU:1, one launch (start us, length us, event | category | flops | bytes accessed | tf_op | source)
XLA Modules:
  0.0 41.8 jit_solution(7711508898868536561)
XLA Ops:
  0.0 40.7 %two_convs.1 = f32[512,512]{1,0:T(8,128)S(1)} custom-call(bf16[4,128,4,128]{3,2,1,0:T(4,128)(2,1)} %bitcast.8, bf16[9,4,512]{2,1,0:T(4,128)(2,1)} %bitcast.9, bf16[4608,512]{1,0:T(8,128)(2,1)} %bitcast.7, f32[1,512]{1,0:T(1,128)} %bitcast.10, f32[1,512]{1,0:T(1,128)} %bitcast.11), custom_call_target="tpu_custom_call" | custom-call | tf_op jit(solution)/shard_map/two_convs/pallas_call | solution.py:401
  40.8 1.0 %arrange.1 = f32[4,16,8,512]{3,2,1,0:T(8,128)} custom-call(f32[8,64,512]{2,1,0:T(8,128)S(1)} %bitcast.6), custom_call_target="tpu_custom_call" | custom-call | tf_op jit(solution)/shard_map/arrange/pallas_call | solution.py:421

commit v22 on v10

--- a/solution.py
+++ b/solution.py
@@ -163,25 +163,32 @@
     last, passed, lent, lent_on = {}, {}, {}, {}
 
     def send_plane(n):
-        last[n] = Step(96, [(piece(p, 2, plane(p, 0), n, core), chip(p, 2, d)) for p in parts for d in (1, 3)])
+        last[n] = [Step(32, [(piece(p, 2, plane(p, 0), n, core), chip(p, 2, d)) for d in (1, 3)]) for p in parts]
 
     def pass_on(n):
-        with jax.named_scope(f"wait_last{n}"):
-            last[n].land()
-        passed[n] = Step(48, [(piece(p, 2, plane(p, 4 - d), n, core, half=d // 2), chip(p, 2, d)) for p in parts for d in (1, 3)]).go()
-        lent[n] = hand_over([piece(p, 2, plane(p, d), n, core) for p in parts for d in (1, 3)], 96)
+        passed[n], lent[n] = {}, {}
+        for p in (1, 2, 0):
+            with jax.named_scope(f"wait_last{n}{p}"):
+                last[n][p].land()
+            on = [(piece(p, 2, plane(p, 4 - d), n, core, half=d // 2), chip(p, 2, d)) for d in (1, 3)]
+            passed[n][p] = Step(16, on).go()
+            lent[n][p] = hand_over([piece(p, 2, plane(p, d), n, core) for d in (1, 3)], 32)
 
     def finish(n):
-        with jax.named_scope(f"wait_passed{n}"):
-            passed[n].land()
-        lent_on[n] = hand_over([piece(p, 2, plane(p, 2), n, core) for p in parts], 48)
+        lent_on[n] = {}
+        for p in (1, 2, 0):
+            with jax.named_scope(f"wait_passed{n}{p}"):
+                passed[n][p].land()
+            lent_on[n][p] = hand_over([piece(p, 2, plane(p, 2), n, core)], 16)
 
     with jax.named_scope("send_third"):
         for n in range(2):
             send_plane(n)
-        last[0].go()
+        for step in last[0]:
+            step.go()
         own = hand_over([piece(p, 2, plane(p, 0), None, core) for p in parts], 96)
-    last[1].go()
+    for step in last[1]:
+        step.go()
     span = got.at[pl.ds(0, 127)]
     everything = pltpu.make_async_remote_copy(
         src_ref=span, dst_ref=span, send_sem=xs_send, recv_sem=xs_recv, device_id=chip(0, 0, 0, 1), device_id_type=MESH
@@ -259,7 +266,8 @@
 
     def near(n):
         with jax.named_scope(f"wait_lent{n}"):
-            lent[n].land()
+            for step in lent[n].values():
+                step.land()
         with jax.named_scope(f"near{n}"):
             for group, top in enumerate(conv1((n,), (3, 1), (inner,), 2)):
                 z_acc[n, pl.ds(5 * group, 5), inner] += top
@@ -274,7 +282,8 @@
 
     def far(n):
         with jax.named_scope(f"wait_lent_on{n}"):
-            lent_on[n].land()
+            for step in lent_on[n].values():
+                step.land()
         lanes = slice(256 * n, 256 * n + 256)
         with jax.named_scope(f"far{n}"):
             for group, top in enumerate(conv1((n,), (2,), (pl.ds(0, 72),), 2)):
@@ -391,8 +400,8 @@
         pltpu.SemaphoreType.DMA,
         pltpu.SemaphoreType.DMA((4,)),
         pltpu.SemaphoreType.DMA((4,)),
-        pltpu.SemaphoreType.DMA((11,)),
-        pltpu.SemaphoreType.DMA((11,)),
+        pltpu.SemaphoreType.DMA((27,)),
+        pltpu.SemaphoreType.DMA((27,)),
     ]
     vmem = pl.BlockSpec(memory_space=pltpu.VMEM)
     anywhere = pl.BlockSpec(memory_space=pl.ANY)

time: 38.7 us -> 38.8 us (level)
  no operation moved by 1% of the time
where the time goes in v22:
time: 38.8 us; the launch traced here: 38.7 us
  Pallas kernels  38.7 us (100%)
    pallas_call x1, Pallas kernels, run_local(): pl.pallas_call(kernel, out_shape=jax.ShapeDtypeStruct((CHANS, CHANS), F32...  37.6 us
    pallas_call x1, Pallas kernels, run_local(): pl.pallas_call(arrange, out_shape=jax.ShapeDtypeStruct((4, 16, 8, CHANS),...  1.05 us

profile of v22, /device:TPU:1, one launch (start us, length us, event | category | flops | bytes accessed | tf_op | source)
XLA Modules:
  0.0 38.7 jit_solution(2683775650406439178)
XLA Ops:
  0.0 37.6 %two_convs.1 = f32[512,512]{1,0:T(8,128)S(1)} custom-call(bf16[4,128,4,128]{3,2,1,0:T(4,128)(2,1)} %bitcast.8, bf16[9,4,512]{2,1,0:T(4,128)(2,1)} %bitcast.9, bf16[4608,512]{1,0:T(8,128)(2,1)} %bitcast.7, f32[1,512]{1,0:T(1,128)} %bitcast.10, f32[1,512]{1,0:T(1,128)} %bitcast.11), custom_call_target="tpu_custom_call" | custom-call | tf_op jit(solution)/shard_map/two_convs/pallas_call | solution.py:410
  37.6 1.0 %arrange.1 = f32[4,16,8,512]{3,2,1,0:T(8,128)} custom-call(f32[8,64,512]{2,1,0:T(8,128)S(1)} %bitcast.6), custom_call_target="tpu_custom_call" | custom-call | tf_op jit(solution)/shard_map/arrange/pallas_call | solution.py:430

commit v23 on v22

--- a/solution.py
+++ b/solution.py
@@ -99,19 +99,18 @@
         pl.semaphore_wait(barrier, 127)
 
     n_steps = [0]
-    steps = []
+    groups = {}
 
     class Step:
-        def __init__(self, slabs, copies):
-            k = n_steps[0]
+        def __init__(self, group, slabs, copies):
+            sent = groups.setdefault(group, [len(groups), 0])
+            sent[1] += slabs
+            self.copies = copies
+            self.sems = dict(
+                send_sem=step_send.at[sent[0]], recv_sem=step_recv.at[n_steps[0]], device_id_type=MESH
+            )
             n_steps[0] += 1
-            sems = dict(send_sem=step_send.at[k], recv_sem=step_recv.at[k], device_id_type=MESH)
-            self.copies, self.sems = copies, sems
-            span = got.at[pl.ds(0, slabs)]
-            self.all = pltpu.make_async_remote_copy(
-                src_ref=span, dst_ref=span, device_id={"model": at_model[0][1], "cols": q}, **sems
-            )
-            steps.append(self)
+            self.slabs = slabs
 
         def go(self):
             for ref, to in self.copies:
@@ -119,7 +118,9 @@
             return self
 
         def land(self):
-            self.all.wait_recv()
+            span = got.at[pl.ds(0, self.slabs)]
+            partner = {"model": at_model[0][1], "cols": q}
+            pltpu.make_async_remote_copy(src_ref=span, dst_ref=span, device_id=partner, **self.sems).wait_recv()
 
     def chip(p, t, d, c=0):
         axis = ORDERS[p][t]
@@ -127,13 +128,13 @@
         return {"model": pos["x"] * 2 + (core + c) % 2, "cols": pos["z"] * 4 + pos["y"]}
 
     def spread(t, slabs):
-        return Step(slabs, [(piece(p, t, me[ORDERS[p][t]], None, core), chip(p, t, d)) for p in parts for d in (1, 3, 2)]).go()
+        return Step(f"spread{t}", slabs, [(piece(p, t, me[ORDERS[p][t]], None, core), chip(p, t, d)) for p in parts for d in (1, 3, 2)]).go()
 
     def plane(p, d):
         return (me[ORDERS[p][2]] + d) % 4
 
-    def hand_over(pieces, slabs):
-        return Step(slabs, [(ref, {"model": at_model[0][1], "cols": q}) for ref in pieces]).go()
+    def hand_over(group, pieces, slabs):
+        return Step(group, slabs, [(ref, {"model": at_model[0][1], "cols": q}) for ref in pieces]).go()
 
     def send_windows(first, last):
         for d in others[first:last]:
@@ -163,30 +164,30 @@
     last, passed, lent, lent_on = {}, {}, {}, {}
 
     def send_plane(n):
-        last[n] = [Step(32, [(piece(p, 2, plane(p, 0), n, core), chip(p, 2, d)) for d in (1, 3)]) for p in parts]
+        last[n] = [Step(f"last{n}", 32, [(piece(p, 2, plane(p, 0), n, core), chip(p, 2, d)) for d in (1, 3)]) for p in parts]
 
     def pass_on(n):
         passed[n], lent[n] = {}, {}
-        for p in (1, 2, 0):
+        for p in (0, 2, 1):
             with jax.named_scope(f"wait_last{n}{p}"):
                 last[n][p].land()
             on = [(piece(p, 2, plane(p, 4 - d), n, core, half=d // 2), chip(p, 2, d)) for d in (1, 3)]
-            passed[n][p] = Step(16, on).go()
-            lent[n][p] = hand_over([piece(p, 2, plane(p, d), n, core) for d in (1, 3)], 32)
+            passed[n][p] = Step(f"passed{n}", 16, on).go()
+            lent[n][p] = hand_over(f"lent{n}", [piece(p, 2, plane(p, d), n, core) for d in (1, 3)], 32)
 
     def finish(n):
         lent_on[n] = {}
         for p in (1, 2, 0):
             with jax.named_scope(f"wait_passed{n}{p}"):
                 passed[n][p].land()
-            lent_on[n][p] = hand_over([piece(p, 2, plane(p, 2), n, core)], 16)
+            lent_on[n][p] = hand_over(f"lent_on{n}", [piece(p, 2, plane(p, 2), n, core)], 16)
 
     with jax.named_scope("send_third"):
         for n in range(2):
             send_plane(n)
         for step in last[0]:
             step.go()
-        own = hand_over([piece(p, 2, plane(p, 0), None, core) for p in parts], 96)
+        own = hand_over("own", [piece(p, 2, plane(p, 0), None, core) for p in parts], 96)
     for step in last[1]:
         step.go()
     span = got.at[pl.ds(0, 127)]
@@ -360,8 +361,17 @@
 
     with jax.named_scope("wait_sends"):
         everything.wait_send()
-        for step in steps:
-            step.all.wait_send()
+        for k, slabs in groups.values():
+            span = got.at[pl.ds(0, slabs)]
+            partner = {"model": at_model[0][1], "cols": q}
+            pltpu.make_async_remote_copy(
+                src_ref=span,
+                dst_ref=span,
+                send_sem=step_send.at[k],
+                recv_sem=step_recv.at[k],
+                device_id=partner,
+                device_id_type=MESH,
+            ).wait_send()
         for copy in halo:
             copy.wait_send()
 
@@ -400,7 +410,7 @@
         pltpu.SemaphoreType.DMA,
         pltpu.SemaphoreType.DMA((4,)),
         pltpu.SemaphoreType.DMA((4,)),
-        pltpu.SemaphoreType.DMA((27,)),
+        pltpu.SemaphoreType.DMA((11,)),
         pltpu.SemaphoreType.DMA((27,)),
     ]
     vmem = pl.BlockSpec(memory_space=pltpu.VMEM)

time: 38.8 us -> 38.7 us (level)
  no operation moved by 1% of the time
where the time goes in v23:
time: 38.7 us; the launch traced here: 38.6 us
  Pallas kernels  38.6 us (100%)
    pallas_call x1, Pallas kernels, run_local(): pl.pallas_call(kernel, out_shape=jax.ShapeDtypeStruct((CHANS, CHANS), F32...  37.6 us
    pallas_call x1, Pallas kernels, run_local(): pl.pallas_call(arrange, out_shape=jax.ShapeDtypeStruct((4, 16, 8, CHANS),...  1.05 us

profile of v23, /device:TPU:1, one launch (start us, length us, event | category | flops | bytes accessed | tf_op | source)
XLA Modules:
  0.0 38.6 jit_solution(17304406826173900722)
XLA Ops:
  0.0 37.6 %two_convs.1 = f32[512,512]{1,0:T(8,128)S(1)} custom-call(bf16[4,128,4,128]{3,2,1,0:T(4,128)(2,1)} %bitcast.8, bf16[9,4,512]{2,1,0:T(4,128)(2,1)} %bitcast.9, bf16[4608,512]{1,0:T(8,128)(2,1)} %bitcast.7, f32[1,512]{1,0:T(1,128)} %bitcast.10, f32[1,512]{1,0:T(1,128)} %bitcast.11), custom_call_target="tpu_custom_call" | custom-call | tf_op jit(solution)/shard_map/two_convs/pallas_call | solution.py:420
  37.6 1.0 %arrange.1 = f32[4,16,8,512]{3,2,1,0:T(8,128)} custom-call(f32[8,64,512]{2,1,0:T(8,128)S(1)} %bitcast.6), custom_call_target="tpu_custom_call" | custom-call | tf_op jit(solution)/shard_map/arrange/pallas_call | solution.py:440
